TPU v7x, 128 devices: a whole 4x4x4 slice. The times are simulated.
128 devices in a mesh: seq: 16 (over x_hi, z, core), tp: 8 (over y, x_lo).
Axes of the slice: x: 4 (x_hi: 2, x_lo: 2; x = x_hi * 2 + x_lo), y: 4, z: 4, core: 2. Of those that a mesh axis runs over, the one named last changes fastest.
Arguments:
- tokens: bfloat16 [2048, 8192], P('seq'), may hold values from -6 to 6
- conv_weight: float32 [4, 8192], replicated, may hold values from -3 to 3
- norm_gain: float32 [8192], replicated, may hold values from 0.25 to 1.75
- gate_weight: bfloat16 [8192, 14336], P('seq', 'tp'), may hold values from -0.0625 to 0.0625
- up_weight: bfloat16 [8192, 14336], P('seq', 'tp'), may hold values from -0.0625 to 0.0625
- down_weight: bfloat16 [14336, 8192], P('tp', 'seq'), may hold values from -0.046875 to 0.046875
Outputs:
- mixed_out: bfloat16 [2048, 8192], P(('seq', 'tp'))
All inputs are finite; a program needn't handle non-finite values.
Results may differ from a plain program's by a relative error of at most 0.03.
Values may be sent and summed in bfloat16 or wider, within the bound.
No kernel may reach another device: no remote copies, remote signals or barrier semaphores. Data moves between devices by JAX's collectives and lax.ppermute only.
A program may use at most 64 MiB of HBM per device.

v0:
```python
import jax
import jax.numpy as jnp
from jax import lax
from jax.sharding import PartitionSpec as P


def from_behind(shard, axis, by):
    peers = lax.axis_size(axis)
    pairs = [(i, i + by) for i in range(peers) if 0 <= i + by < peers]
    return lax.ppermute(shard, axis, pairs)


def split_up(shard, dim, peers):
    shape = shard.shape
    parts = shard.reshape(*shape[:dim], peers, shape[dim] // peers, *shape[dim + 1 :])
    return jnp.moveaxis(parts, dim, 0)


def summed_on_arrival(shard, axis, dim):
    parts = split_up(shard, dim, lax.axis_size(axis))
    arrived = lax.all_to_all(parts, axis, split_axis=0, concat_axis=0, tiled=True)
    return arrived.astype(jnp.float32).sum(axis=0)


def swiglu(both_sums, half_cols):
    return (jax.nn.silu(both_sums[:, :half_cols]) * both_sums[:, half_cols:]).astype(jnp.bfloat16)


def shards(tokens, conv_weight, norm_gain, gate_weight, up_weight, down_weight):
    tok_rows = tokens.shape[0]
    taps_count = conv_weight.shape[0]
    seq_count = lax.axis_size("seq")
    edge_rows = from_behind(tokens[tok_rows - (taps_count - 1) :], "seq", 1)
    extended = jnp.concatenate([edge_rows, tokens], 0).astype(jnp.float32)
    conv_out = jnp.zeros(tokens.shape, jnp.float32)
    for tap_index in range(taps_count):
        begin = taps_count - 1 - tap_index
        conv_out = conv_out + conv_weight[tap_index][None, :] * extended[begin : begin + tok_rows]
    scale_rms = lax.rsqrt(jnp.mean(conv_out * conv_out, axis=-1, keepdims=True) + 1e-05)
    normed = (conv_out * scale_rms * norm_gain[None, :]).astype(jnp.bfloat16)
    all_rows = lax.all_to_all(normed, "seq", split_axis=1, concat_axis=0, tiled=True)
    half_cols = gate_weight.shape[1]
    w_both = jnp.concatenate([gate_weight, up_weight], 1)
    gate_share = lax.psum_scatter(
        jnp.dot(all_rows, w_both, preferred_element_type=jnp.float32).astype(jnp.bfloat16),
        "seq",
        scatter_dimension=0,
        tiled=True,
    ).astype(jnp.float32)
    hidden = swiglu(gate_share, half_cols)
    out_terms = jnp.dot(
        lax.all_gather(hidden, "seq", axis=0, tiled=True),
        down_weight,
        preferred_element_type=jnp.float32,
    )
    col_width = out_terms.shape[1]
    out_terms = out_terms.reshape(seq_count, tok_rows, col_width)
    summed = summed_on_arrival(out_terms.astype(jnp.bfloat16), "tp", 1)
    rounded = summed.astype(jnp.bfloat16)
    mixed_out = lax.all_to_all(rounded, "seq", split_axis=0, concat_axis=2, tiled=True)
    return mixed_out.reshape(mixed_out.shape[1], mixed_out.shape[2])


def solution(mesh):
    in_specs = (P("seq", None), P(), P(), P("seq", "tp"), P("seq", "tp"), P("tp", "seq"))
    out_specs = P(("seq", "tp"), None)
    return jax.shard_map(shards, mesh=mesh, in_specs=in_specs, out_specs=out_specs, check_vma=False)
```

profile of v0, /device:TPU:1, one launch (start us, length us, event | category | flops | bytes accessed | tf_op | source)
XLA Modules:
  0.0 350.1 jit_solution(9454202880680602987)
XLA Ops:
  6.5 0.0 copy-start
  6.5 0.0 reduce-scatter.2.cloned.1.call-start
  6.5 1.1 slice.34
  7.6 4.9 %collective-permute-start = (bf16[3,8192]{1,0:T(4,128)(2,1)S(1)}, bf16[3,8192]{1,0:T(4,128)(2,1)S(1)}, u32[]{:S(2)}, u32[]{:S(2)}) collective-permute-start(bf16[3,8192]{1,0:T(4,128)(2,1)S(1)} %slice.34), channel_id=1, source_target_pairs={{0,8},{8,16},{16,24},{24,32},{32,40},{40,48},{48,56},{56,64},{64,7... | collective-permute-start | bytes 147464 | tf_op jit(solution)/shard_map/ppermute | solution.py:10
  12.5 1.4 fusion.9
  13.9 4.1 %copy.16 = bf16[128,8192]{0,1:T(8,128)(2,1)} copy(bf16[128,8192]{1,0:T(8,128)(2,1)} %param.6) | data formatting | bytes 4194304 | tf_op args[0]
  18.0 0.0 collective-permute-done
  18.0 1.8 copy.15
  19.8 3.7 %maximum_convert_fusion = f32[131,8192]{0,1:T(8,128)S(1)} fusion(bf16[128,8192]{0,1:T(8,128)(2,1)} %copy.16, bf16[3,8192]{0,1:T(8,128)(2,1)} %copy.15), kind=kLoop, calls=%fused_computation.8 | loop fusion | flops 4292608 | bytes 6438912 | tf_op jit(solution)/shard_map/convert_element_type | solution.py:34
  23.6 0.0 copy-start.1
  23.6 8.7 %multiply_reduce_fusion = (f32[128]{0:T(128)S(1)}, f32[128,8192]{0,1:T(8,128)S(1)}) fusion(f32[131,8192]{0,1:T(8,128)S(1)} %maximum_convert_fusion, f32[8192]{0:T(1024)S(1)} %bitcast.30, f32[8192]{0:T(1024)S(1)} %bitcast.31, f32[8192]{0:T(1024)S(1)} %bitcast.29, f32[8192]{0:T(1024)S(1)} %bitcast.28), kind=kLoop, calls=%fused_computation.10 | loop fusion | flops 9437056 | bytes 21103104 | tf_op jit(solution)/shard_map/reduce_sum | solution.py:39
  32.3 0.0 copy-done.1
  32.3 3.5 multiply_convert_fusion
  35.8 35.4 %all_to_all.39 = bf16[128,16,512]{0,2,1:T(8,128)(2,1)} all-to-all(bf16[128,16,512]{0,2,1:T(8,128)(2,1)S(1)} %bitcast.22), channel_id=1, replica_groups=mesh['seq'=16,'tp'=8] {'seq'}, dimensions={1} | all-to-all | bytes 4194304 | tf_op jit(solution)/shard_map/all_to_all | solution.py:41
  71.2 3.9 %copy.17 = bf16[16,128,512]{2,1,0:T(8,128)(2,1)} copy(bf16[16,128,512]{1,2,0:T(8,128)(2,1)} %bitcast.23) | data formatting | bytes 4194304 | tf_op jit(solution)/shard_map/all_to_all | solution.py:41
  75.1 13.4 %convolution_convert_fusion = bf16[2048,3584]{1,0:T(8,128)(2,1)} fusion(bf16[2048,512]{1,0:T(8,128)(2,1)} %bitcast.25, bf16[512,1792]{1,0:T(8,128)(2,1)} %param.10, bf16[512,1792]{1,0:T(8,128)(2,1)} %param.9), kind=kOutput, calls=%fused_computation | convolution fusion | flops 7530872832 | bytes 20447232 | tf_op jit(solution)/shard_map/dot_general | solution.py:45
  88.5 0.0 reduce-scatter.2.cloned.1.call-update
  88.5 0.0 all-gather.2.cloned.1.call-start
  88.6 129.9 %reduce-scatter.2.cloned.1.call-done = bf16[128,3584]{1,0:T(8,128)(2,1)} async-done(((bf16[2048,3584]{1,0:T(8,128)(2,1)}), bf16[128,3584]{1,0:T(8,128)(2,1)}) %reduce-scatter.2.cloned.1.call-update) | async-done | bytes 917520 | tf_op jit(solution)/shard_map/reduce_scatter | solution.py:44
  218.4 1.4 convert_element_type.27
  219.8 1.0 fusion.6
  220.8 0.0 all-gather.2.cloned.1.call-update
  220.8 67.8 %all-gather.2.cloned.1.call-done = bf16[2048,1792]{1,0:T(8,128)(2,1)} async-done(((bf16[128,1792]{1,0:T(8,128)(2,1)}), bf16[2048,1792]{1,0:T(8,128)(2,1)}) %all-gather.2.cloned.1.call-update) | async-done | bytes 7340048 | tf_op jit(solution)/shard_map/all_gather | solution.py:52
  288.6 0.0 copy-done
  288.7 7.3 %convolution_convert_fusion.1 = bf16[2048,512]{1,0:T(8,128)(2,1)S(1)} fusion(bf16[2048,1792]{1,0:T(8,128)(2,1)} %all-gather.2.cloned.1.call-done, bf16[1792,512]{1,0:T(8,128)(2,1)S(1)} %copy-done), kind=kOutput, calls=%fused_computation.14 | convolution fusion | flops 3759144960 | bytes 11272192 | tf_op jit(solution)/shard_map/dot_general | solution.py:51
  295.9 0.2 copy.25
  296.1 30.1 %all_to_all.40 = bf16[8,16,16,512]{3,2,1,0:T(8,128)(2,1)} all-to-all(bf16[8,16,16,512]{3,2,1,0:T(8,128)(2,1)S(1)} %bitcast.24), channel_id=1, replica_groups=mesh['seq'=16,'tp'=8] {'tp'}, dimensions={0} | all-to-all | bytes 4194304 | tf_op jit(solution)/shard_map/all_to_all | solution.py:21
  326.2 2.0 reduce_sum.22
  328.2 14.4 %all_to_all.41 = bf16[16,16,512]{2,1,0:T(8,128)(2,1)S(1)} all-to-all(bf16[16,16,512]{2,1,0:T(8,128)(2,1)S(1)} %reduce_sum.22), channel_id=1, replica_groups=mesh['seq'=16,'tp'=8] {'seq'}, dimensions={0} | all-to-all | bytes 524288 | tf_op jit(solution)/shard_map/all_to_all | solution.py:60
  342.6 0.7 copy.22
  (1 shorter events, 0.0 us)
Async XLA Ops:
  6.5 282.1 %copy-start = (bf16[1792,512]{1,0:T(8,128)(2,1)S(1)}, bf16[1792,512]{1,0:T(8,128)(2,1)}, u32[]{:S(2)}) copy-start(bf16[1792,512]{1,0:T(8,128)(2,1)} %param.11) | copy-start | bytes 5505028
  6.5 211.9 %reduce-scatter.2.cloned.1.call-start = ((), (), s32[]{:S(2)}) async-start(), calls=%async_computation.4 | async-start | bytes 15597568 | tf_op jit(solution)/shard_map/reduce_scatter | solution.py:44
  7.6 10.4 %collective-permute-start = (bf16[3,8192]{1,0:T(4,128)(2,1)S(1)}, bf16[3,8192]{1,0:T(4,128)(2,1)S(1)}, u32[]{:S(2)}, u32[]{:S(2)}) collective-permute-start(bf16[3,8192]{1,0:T(4,128)(2,1)S(1)} %slice.34), channel_id=1, source_target_pairs={{0,8},{8,16},{16,24},{24,32},{32,40},{40,48},{48,56},{56,64},{64,7... | collective-permute-start | bytes 147464 | tf_op jit(solution)/shard_map/ppermute | solution.py:10
  23.6 8.8 %copy-start.1 = (f32[8192]{0:T(1024)S(1)}, f32[8192]{0:T(1024)}, u32[]{:S(2)}) copy-start(f32[8192]{0:T(1024)} %param.8) | copy-start | bytes 98308
  88.5 200.1 %all-gather.2.cloned.1.call-start = ((), (), s32[]{:S(2)}) async-start(), calls=%async_computation.5 | async-start | bytes 7798784 | tf_op jit(solution)/shard_map/all_gather | solution.py:52
Sparse Core Ops, SparseCore 0:
  88.6 129.7 reduce-scatter.1
  221.0 67.6 all-gather.1
where the time goes:
time: 351 us; the launch traced here: 350 us
  waiting for transfers between devices  198 us (56%)
  blocking collectives  79.8 us (23%)
  matrix products  20.6 us (6%)
  other arithmetic  20.3 us (6%)
  between operations  13.5 us (4%)
  local copies, waits for them, and re-layouts  13.2 us (4%)
  starting transfers between devices  4.97 us (1%)
    reduce_scatter x1, waiting for transfers between devices, shards(): lax.psum_scatter(jnp.dot(all_rows, w_both, preferred_element_type=jnp.flo...  130 us
    all_gather x1, waiting for transfers between devices, shards(): lax.all_gather(hidden, 'seq', axis=0, tiled=True)  67.8 us
    all_to_all x1, blocking collectives, shards(): lax.all_to_all(normed, 'seq', split_axis=1, concat_axis=0, tiled=True)  35.4 us
    all_to_all x1, blocking collectives, summed_on_arrival(): lax.all_to_all(parts, axis, split_axis=0, concat_axis=0, tiled=True)  30.1 us
    all_to_all x1, blocking collectives, shards(): lax.all_to_all(rounded, 'seq', split_axis=0, concat_axis=2, tiled=True)  14.4 us
    dot_general x1, matrix products, shards(): jnp.dot(all_rows, w_both, preferred_element_type=jnp.float32)  13.4 us
    reduce_sum x1, other arithmetic, shards(): jnp.mean(conv_out * conv_out, axis=-1, keepdims=True) + 1e-05  8.75 us
    dot_general x1, matrix products, shards(): jnp.dot(lax.all_gather(hidden, 'seq', axis=0, tiled=True), down_weight, p...  7.26 us
  transfers between devices with their start and end apart: 3, of which 2 were waited for; matrix products, arithmetic and copies ran while one was open for 2% of the time, Pallas kernels for 0%

commit v1 on v0

v1 whole, which is shorter than its diff:
```python
import jax
import jax.numpy as jnp
import numpy as np
from jax import lax
from jax.experimental import pallas as pl
from jax.experimental.pallas import tpu as pltpu
from jax.sharding import Mesh, PartitionSpec as P

CHIPS = ("xh", "z")
TP = ("y", "xl")
SEQ = ("xh", "z", "c")
BF16, F32 = jnp.bfloat16, jnp.float32


def conv_norm(tokens, edge, conv_weight, gain, peers):
    rows, width = tokens.shape
    taps = conv_weight.shape[0]
    group = width // peers
    step = 16
    lanes = 512
    pad = edge.shape[0]

    def body(tok, edg, cw, gn, out, ext, conv):
        i = pl.program_id(0)

        @pl.when(i == 0)
        def _():
            ext[:pad] = edg[...].astype(F32)

        @pl.when(i > 0)
        def _():
            ext[:pad] = ext[step : step + pad]

        ext[pad:] = tok[...].astype(F32)
        squares = jnp.zeros((step, 128), F32)
        for p in range(width // lanes):
            at = slice(p * lanes, (p + 1) * lanes)
            acc = cw[0:1, at] * ext[pad : pad + step, at]
            for k in range(1, taps):
                acc = acc + cw[k : k + 1, at] * ext[pad - k : pad - k + step, at]
            conv[:, at] = acc
            for j in range(lanes // 128):
                piece = acc[:, j * 128 : (j + 1) * 128]
                squares = squares + piece * piece
        mean = jnp.sum(squares, axis=1, keepdims=True) * (1.0 / width)
        scale = lax.rsqrt(mean + 1e-05)
        for p in range(width // lanes):
            at = slice(p * lanes, (p + 1) * lanes)
            lo = p * lanes % group
            out[p * lanes // group, :, lo : lo + lanes] = (conv[:, at] * scale * gn[:, at]).astype(BF16)

    return pl.pallas_call(
        body,
        grid=(rows // step,),
        in_specs=[
            pl.BlockSpec((step, width), lambda i: (i, 0)),
            pl.BlockSpec((pad, width), lambda i: (0, 0)),
            pl.BlockSpec((taps, width), lambda i: (0, 0)),
            pl.BlockSpec((1, width), lambda i: (0, 0)),
        ],
        out_specs=pl.BlockSpec((peers, step, group), lambda i: (0, i, 0)),
        out_shape=jax.ShapeDtypeStruct((peers, rows, group), BF16),
        scratch_shapes=[pltpu.VMEM((pad + step, width), F32), pltpu.VMEM((step, width), F32)],
        compiler_params=pltpu.CompilerParams(dimension_semantics=("arbitrary",)),
        name="conv_norm",
    )(tokens, edge, conv_weight, gain)


def gate_up(core, x, own_gate, other_gate, own_up, other_up, blocks):
    rows, depth = x.shape
    half, cols = own_gate.shape
    per = rows // blocks
    tile = 256

    def body(core_ref, x_ref, g0, g1, u0, u1, out):
        c = core_ref[0]
        mine = x_ref[:, pl.ds(pl.multiple_of(c * half, half), half)]
        theirs = x_ref[:, pl.ds(pl.multiple_of((1 - c) * half, half), half)]
        for k, (a, b) in enumerate(((g0, g1), (u0, u1))):
            total = jnp.dot(mine, a[...], preferred_element_type=F32) + jnp.dot(
                theirs, b[...], preferred_element_type=F32
            )
            out[:, k] = total.astype(BF16).reshape(blocks, per, tile)

    weight = pl.BlockSpec((half, tile), lambda n, c: (0, n))
    return pl.pallas_call(
        body,
        grid_spec=pltpu.PrefetchScalarGridSpec(
            num_scalar_prefetch=1,
            grid=(cols // tile,),
            in_specs=[pl.BlockSpec((rows, depth), lambda n, c: (0, 0))] + [weight] * 4,
            out_specs=pl.BlockSpec((blocks, 2, per, tile), lambda n, c: (0, 0, 0, n)),
        ),
        out_shape=jax.ShapeDtypeStruct((blocks, 2, per, cols), BF16),
        compiler_params=pltpu.CompilerParams(dimension_semantics=("arbitrary",)),
        name="gate_up",
    )(core, x, own_gate, other_gate, own_up, other_up)


def down(core, hidden, own, other, blocks, parts):
    rows, depth = hidden.shape
    half = own.shape[1]
    per = rows // blocks
    sub = per // parts

    def body(core_ref, h, d0, d1, out):
        c = core_ref[0]
        for at, w in ((c, d0), (1 - c, d1)):
            total = jnp.dot(h[...], w[...], preferred_element_type=F32).astype(BF16)
            out[:, 0, :, pl.ds(pl.multiple_of(at * half, half), half)] = total.reshape(parts, sub, half)

    return pl.pallas_call(
        body,
        grid_spec=pltpu.PrefetchScalarGridSpec(
            num_scalar_prefetch=1,
            grid=(blocks,),
            in_specs=[
                pl.BlockSpec((per, depth), lambda b, c: (b, 0)),
                pl.BlockSpec((depth, half), lambda b, c: (0, 0)),
                pl.BlockSpec((depth, half), lambda b, c: (0, 0)),
            ],
            out_specs=pl.BlockSpec((parts, 1, sub, 2 * half), lambda b, c: (0, b, 0, 0)),
        ),
        out_shape=jax.ShapeDtypeStruct((parts, blocks, sub, 2 * half), BF16),
        compiler_params=pltpu.CompilerParams(dimension_semantics=("arbitrary",)),
        name="down",
    )(core, hidden, own, other)


def shards(tokens, conv_weight, norm_gain, gate_weight, up_weight, down_weight):
    chips = lax.axis_size(CHIPS)
    parts = lax.axis_size(TP)
    seq = lax.axis_size(SEQ)
    core = lax.axis_index("c").astype(jnp.int32).reshape(1)
    swap = lambda w: lax.ppermute(w, "c", [(0, 1), (1, 0)])
    edge = lax.ppermute(tokens[-8:], SEQ, [(i, i + 1) for i in range(seq - 1)])
    gate_other, up_other, down_other = swap(gate_weight), swap(up_weight), swap(down_weight)
    normed = conv_norm(tokens, edge, conv_weight, norm_gain[None, :], chips)
    rows = lax.all_to_all(normed, CHIPS, split_axis=0, concat_axis=0, tiled=True)
    rows = rows.reshape(-1, rows.shape[2])
    sums = gate_up(core, rows, gate_weight, gate_other, up_weight, up_other, chips)
    mine = lax.psum_scatter(sums, CHIPS, scatter_dimension=0, tiled=True)[0].astype(F32)
    hidden = (jax.nn.silu(mine[0]) * mine[1]).astype(BF16)
    everyone = lax.all_gather(hidden, CHIPS, axis=0, tiled=True)
    terms = down(core, everyone, down_weight, down_other, chips, parts)
    arrived = lax.all_to_all(terms, TP, split_axis=0, concat_axis=0, tiled=True)
    summed = arrived.astype(F32).sum(axis=0).astype(BF16)
    out = lax.all_to_all(summed, CHIPS, split_axis=0, concat_axis=0, tiled=True)
    return jnp.transpose(out, (1, 0, 2)).reshape(out.shape[1], -1)


def solution(mesh):
    fine = Mesh(np.asarray(mesh.devices).reshape(2, 4, 2, 4, 2), ("xh", "z", "c", "y", "xl"))
    in_specs = (P(SEQ, None), P(), P(), P(SEQ, TP), P(SEQ, TP), P(TP, SEQ))
    out_specs = P(SEQ + TP, None)
    return jax.shard_map(shards, mesh=fine, in_specs=in_specs, out_specs=out_specs, check_vma=False)
```

time: 351 us -> 305 us (0.87)
  blocking collectives: 79.8 us -> 40.7 us
  Pallas kernels: 0 us -> 30.1 us
  matrix products: 20.6 us -> 0 us
  other arithmetic: 20.3 us -> 2.7 us
  starting transfers between devices: 4.97 us -> 14.2 us
  local copies, waits for them, and re-layouts: 13.2 us -> 4.28 us
    all_to_all x3 -> x2, blocking collectives: 79.8 us -> 40.7 us  [the longest x1 29.3 us: shards(): arrived = lax.all_to_all(terms, TP, split_axis=0, concat_axis=0, tiled=True)]
    pallas_call x0 -> x3, Pallas kernels: none -> 30.1 us  [the longest x1 12.9 us: gate_up(): pl.pallas_call(body, grid_spec=pltpu.PrefetchScalarGridSpec(num_scalar_pr...]
    all_to_all x0 -> x1, waiting for transfers between devices: none -> 26.1 us  [shards(): lax.all_to_all(normed, CHIPS, split_axis=0, concat_axis=0, tiled=True)]
    reduce_scatter x1, waiting for transfers between devices: 130 us -> 105 us  [shards(): lax.psum_scatter(sums, CHIPS, scatter_dimension=0, tiled=True)[0]]
    dot_general x2 -> x0, matrix products: 20.6 us -> none  [the longest x1 13.4 us: shards(): jnp.dot(all_rows, w_both, preferred_element_type=jnp.float32)]
    reduce_sum x2 -> x1, other arithmetic: 10.7 us -> 0.37 us  [shards(): summed = arrived.astype(F32).sum(axis=0).astype(BF16)]
    all_gather x1, waiting for transfers between devices: 67.8 us -> 59.5 us  [shards(): everyone = lax.all_gather(hidden, CHIPS, axis=0, tiled=True)]
    convert_element_type x4 -> x2, other arithmetic: 9.58 us -> 2.33 us  [the longest x1 1.3 us: shards(): lax.psum_scatter(sums, CHIPS, scatter_dimension=0, tiled=True)[0]]
  transfers between devices with their start and end apart: 3 -> 7, of which waited for: 2 -> 5; matrix products, arithmetic and copies ran while one was open for 2% -> 0% of each run, Pallas kernels for 0% -> 3%
where the time goes in v1:
time: 305 us; the launch traced here: 301 us
  waiting for transfers between devices  196 us (64%)
  blocking collectives  40.7 us (13%)
  Pallas kernels  30.1 us (10%)
  starting transfers between devices  14.2 us (5%)
  between operations  13.5 us (4%)
  local copies, waits for them, and re-layouts  4.28 us (1%)
    reduce_scatter x1, waiting for transfers between devices, shards(): lax.psum_scatter(sums, CHIPS, scatter_dimension=0, tiled=True)[0]  105 us
    all_gather x1, waiting for transfers between devices, shards(): everyone = lax.all_gather(hidden, CHIPS, axis=0, tiled=True)  59.5 us
    all_to_all x1, blocking collectives, shards(): arrived = lax.all_to_all(terms, TP, split_axis=0, concat_axis=0, tiled=True)  29.3 us
    all_to_all x1, waiting for transfers between devices, shards(): lax.all_to_all(normed, CHIPS, split_axis=0, concat_axis=0, tiled=True)  26.1 us
    pallas_call x1, Pallas kernels, gate_up(): pl.pallas_call(body, grid_spec=pltpu.PrefetchScalarGridSpec(num_scalar_pr...  12.9 us
    all_to_all x1, blocking collectives, shards(): out = lax.all_to_all(summed, CHIPS, split_axis=0, concat_axis=0, tiled=True)  11.4 us
    pallas_call x1, Pallas kernels, down(): pl.pallas_call(body, grid_spec=pltpu.PrefetchScalarGridSpec(num_scalar_pr...  9.66 us
    pallas_call x1, Pallas kernels, conv_norm(): pl.pallas_call(body, grid=(rows // step,), in_specs=[pl.BlockSpec((step,...  7.57 us
  transfers between devices with their start and end apart: 7, of which 5 were waited for; matrix products, arithmetic and copies ran while one was open for 0% of the time, Pallas kernels for 3%

profile of v1, /device:TPU:1, one launch (start us, length us, event | category | flops | bytes accessed | tf_op | source)
XLA Modules:
  0.0 301.2 jit_solution(8272286823505652863)
XLA Ops:
  6.5 0.9 slice.11
  7.5 4.9 %collective-permute-start = (bf16[8,8192]{1,0:T(8,128)(2,1)S(1)}, bf16[8,8192]{1,0:T(8,128)(2,1)S(1)}, u32[]{:S(2)}, u32[]{:S(2)}) collective-permute-start(bf16[8,8192]{1,0:T(8,128)(2,1)S(1)} %slice.11), channel_id=1, source_target_pairs={{0,8},{8,16},{16,24},{24,32},{32,40},{40,48},{48,56},{56,64},{64,7... | collective-permute-start | bytes 393224 | tf_op jit(solution)/shard_map/ppermute | solution.py:136
  12.4 0.1 collective-permute-start.1
  12.5 0.5 collective-permute-start.2
  13.0 1.3 collective-permute-done.edg
  14.3 0.0 copy-start.2
  14.3 0.7 copy-done.2
  15.0 7.6 %conv_norm.1 = bf16[8,128,1024]{2,1,0:T(8,128)(2,1)} custom-call(bf16[128,8192]{1,0:T(8,128)(2,1)} %tok.1, bf16[8,8192]{1,0:T(8,128)(2,1)} %copy-done.2, f32[4,8192]{1,0:T(4,128)} %cw.1, f32[1,8192]{1,0:T(1,128)} %bitcast.18), custom_call_target="tpu_custom_call" | custom-call | tf_op jit(solution)/shard_map/conv_norm/pallas_call | solution.py:52
  22.5 7.0 %all-to-all-start = ((bf16[8,128,1024]{2,1,0:T(8,128)(2,1)}), bf16[8,128,1024]{2,1,0:T(8,128)(2,1)S(1)}, u32[]{:S(2)}, u32[]{:S(2)}) async-start(bf16[8,128,1024]{2,1,0:T(8,128)(2,1)} %conv_norm.1), calls=%async_computation | async-start | bytes 4194304 | tf_op jit(solution)/shard_map/all_to_all | solution.py:139
  29.6 0.0 reduce-scatter.2.cloned.1.call-start
  29.6 0.0 collective-permute-done.1.g1
  29.6 0.0 collective-permute-done.2.u1
  29.6 26.1 %all-to-all-done = bf16[8,128,1024]{2,1,0:T(8,128)(2,1)S(1)} async-done(((bf16[8,128,1024]{2,1,0:T(8,128)(2,1)}), bf16[8,128,1024]{2,1,0:T(8,128)(2,1)S(1)}, u32[]{:S(2)}, u32[]{:S(2)}) %all-to-all-start) | async-done | bytes 2097184 | tf_op jit(solution)/shard_map/all_to_all | solution.py:139
  55.8 0.0 copy-start
  55.8 1.4 copy-done
  57.2 12.9 %gate_up.1 = bf16[8,2,128,1792]{3,2,1,0:T(8,128)(2,1)} custom-call(s32[1]{0:T(128)} %bitcast.core_ref, bf16[1024,1024]{1,0:T(8,128)(2,1)} %bitcast.16, bf16[512,1792]{1,0:T(8,128)(2,1)} %g0.1, bf16[512,1792]{1,0:T(8,128)(2,1)} %collective-permute-done.1.g1, bf16[512,1792]{1,0:T(8,128)(2,1)} %u0.1, bf16[512,1792]{1,0:T(8,128)(2,1)} %collective-permute-done.2.u1), custom_call_target="tpu_custom_call" | custom-call | tf_op jit(solution)/shard_map/gate_up/pallas_call | solution.py:86
  70.1 0.0 reduce-scatter.2.cloned.1.call-update
  70.1 0.0 all-gather.2.cloned.1.call-start
  70.2 105.1 %reduce-scatter.2.cloned.1.call-done = bf16[1,2,128,1792]{3,2,1,0:T(8,128)(2,1)} async-done(((bf16[8,2,128,1792]{3,2,1,0:T(8,128)(2,1)}), bf16[1,2,128,1792]{3,2,1,0:T(8,128)(2,1)}) %reduce-scatter.2.cloned.1.call-update) | async-done | bytes 917520 | tf_op jit(solution)/shard_map/reduce_scatter | solution.py:142
  175.3 1.3 convert_element_type.9
  176.6 0.0 copy-start.1
  176.6 1.0 fusion.1
  177.6 0.0 all-gather.2.cloned.1.call-update
  177.7 0.6 copy-done.1
  178.3 1.5 collective-permute-start.3
  179.8 3.5 %collective-permute-done.3.d1 = bf16[1792,512]{1,0:T(8,128)(2,1)} collective-permute-done((bf16[1792,512]{1,0:T(8,128)(2,1)S(1)}, bf16[1792,512]{1,0:T(8,128)(2,1)}, u32[]{:S(2)}, u32[]{:S(2)}) %collective-permute-start.3) | collective-permute-done | bytes 1835040 | tf_op jit(solution)/shard_map/ppermute | solution.py:135
  183.3 59.5 %all-gather.2.cloned.1.call-done.h = bf16[1024,1792]{1,0:T(8,128)(2,1)} async-done(((bf16[128,1792]{1,0:T(8,128)(2,1)}), bf16[1024,1792]{1,0:T(8,128)(2,1)}) %all-gather.2.cloned.1.call-update) | async-done | bytes 3670032 | tf_op jit(solution)/shard_map/all_gather | solution.py:144
  242.9 9.7 %down.1 = bf16[8,8,16,1024]{3,2,1,0:T(8,128)(2,1)} custom-call(s32[1]{0:T(128)} %bitcast.core_ref, bf16[1024,1792]{1,0:T(8,128)(2,1)} %all-gather.2.cloned.1.call-done.h, bf16[1792,512]{1,0:T(8,128)(2,1)} %d0.1, bf16[1792,512]{1,0:T(8,128)(2,1)} %collective-permute-done.3.d1), custom_call_target="tpu_custom_call" | custom-call | tf_op jit(solution)/shard_map/down/pallas_call | solution.py:112
  252.5 29.3 %all_to_all.15 = bf16[8,8,16,1024]{3,2,1,0:T(8,128)(2,1)S(1)} all-to-all(bf16[8,8,16,1024]{3,2,1,0:T(8,128)(2,1)} %down.1), channel_id=1, replica_groups=mesh['xh'=2,'z'=4,'c'=2,'y'=4,'xl'=2] {'y','xl'}, dimensions={0} | all-to-all | bytes 4194304 | tf_op jit(solution)/shard_map/all_to_all | solution.py:146
  281.9 0.4 reduce_sum.12
  282.3 11.4 %all_to_all.16 = bf16[8,16,1024]{2,1,0:T(8,128)(2,1)S(1)} all-to-all(bf16[8,16,1024]{2,1,0:T(8,128)(2,1)S(1)} %reduce_sum.12), channel_id=1, replica_groups=mesh['xh'=2,'z'=4,'c'=2,'y'=4,'xl'=2] {'xh','z'}, dimensions={0} | all-to-all | bytes 524288 | tf_op jit(solution)/shard_map/all_to_all | solution.py:148
  293.6 0.7 copy.8
Async XLA Ops:
  7.5 6.9 %collective-permute-start = (bf16[8,8192]{1,0:T(8,128)(2,1)S(1)}, bf16[8,8192]{1,0:T(8,128)(2,1)S(1)}, u32[]{:S(2)}, u32[]{:S(2)}) collective-permute-start(bf16[8,8192]{1,0:T(8,128)(2,1)S(1)} %slice.11), channel_id=1, source_target_pairs={{0,8},{8,16},{16,24},{24,32},{32,40},{40,48},{48,56},{56,64},{64,7... | collective-permute-start | bytes 393224 | tf_op jit(solution)/shard_map/ppermute | solution.py:136
  12.4 17.2 %collective-permute-start.1 = (bf16[512,1792]{1,0:T(8,128)(2,1)}, bf16[512,1792]{1,0:T(8,128)(2,1)}, u32[]{:S(2)}, u32[]{:S(2)}) collective-permute-start(bf16[512,1792]{1,0:T(8,128)(2,1)} %g0.1), channel_id=1, source_target_pairs={{0,8},{8,0},{1,9},{9,1},{2,10},{10,2},{3,11},{11,3},{4,12},{12,4},... | collective-permute-start | bytes 5505032 | tf_op jit(solution)/shard_map/ppermute | solution.py:135
  12.5 17.2 %collective-permute-start.2 = (bf16[512,1792]{1,0:T(8,128)(2,1)}, bf16[512,1792]{1,0:T(8,128)(2,1)}, u32[]{:S(2)}, u32[]{:S(2)}) collective-permute-start(bf16[512,1792]{1,0:T(8,128)(2,1)} %u0.1), channel_id=1, source_target_pairs={{0,8},{8,0},{1,9},{9,1},{2,10},{10,2},{3,11},{11,3},{4,12},{12,4},... | collective-permute-start | bytes 5505032 | tf_op jit(solution)/shard_map/ppermute | solution.py:135
  14.3 0.7 copy-start.2
  22.5 33.2 %all-to-all-start = ((bf16[8,128,1024]{2,1,0:T(8,128)(2,1)}), bf16[8,128,1024]{2,1,0:T(8,128)(2,1)S(1)}, u32[]{:S(2)}, u32[]{:S(2)}) async-start(bf16[8,128,1024]{2,1,0:T(8,128)(2,1)} %conv_norm.1), calls=%async_computation | async-start | bytes 4194304 | tf_op jit(solution)/shard_map/all_to_all | solution.py:139
  29.6 145.7 %reduce-scatter.2.cloned.1.call-start = ((), (), s32[]{:S(2)}) async-start(), calls=%async_computation.4 | async-start | bytes 8257536 | tf_op jit(solution)/shard_map/reduce_scatter | solution.py:142
  55.8 1.4 copy-start
  70.1 172.8 %all-gather.2.cloned.1.call-start = ((), (), s32[]{:S(2)}) async-start(), calls=%async_computation.5 | async-start | bytes 4128768 | tf_op jit(solution)/shard_map/all_gather | solution.py:144
  176.6 1.7 copy-start.1
  178.3 5.1 %collective-permute-start.3 = (bf16[1792,512]{1,0:T(8,128)(2,1)S(1)}, bf16[1792,512]{1,0:T(8,128)(2,1)}, u32[]{:S(2)}, u32[]{:S(2)}) collective-permute-start(bf16[1792,512]{1,0:T(8,128)(2,1)S(1)} %copy-done.1), channel_id=1, source_target_pairs={{0,8},{8,0},{1,9},{9,1},{2,10},{10,2},{3,11},{11,3},{4,12},{12,4},... | collective-permute-start | bytes 5505032 | tf_op jit(solution)/shard_map/ppermute | solution.py:135
Sparse Core Ops, SparseCore 0:
  70.2 105.0 reduce-scatter.1
  177.8 65.0 all-gather.1

commit v2 on v1

v2 whole, which is shorter than its diff:
```python
import jax
import jax.numpy as jnp
import numpy as np
from jax import lax
from jax.experimental import pallas as pl
from jax.experimental.pallas import tpu as pltpu
from jax.sharding import Mesh, PartitionSpec as P


CHIPS = ("xh", "z")
TP = ("y", "xl")
SEQ = ("xh", "z", "c")
SHAPE = {"xh": 2, "z": 4, "c": 2, "y": 4, "xl": 2}
STEPS = (0, 1, 3, 2)
PEERS = ((1, 0), (0, 3), (1, 3), (0, 1), (1, 1), (0, 2), (1, 2))
BF16, F32 = jnp.bfloat16, jnp.float32


def hop(x, dx, dz):
    pairs = []
    for a in range(SHAPE["xh"]):
        for b in range(SHAPE["z"]):
            pairs.append((a * 4 + b, (a + dx) % 2 * 4 + (b + dz) % 4))
    return lax.ppermute(x, CHIPS, pairs)


def conv_norm(place, tokens, edge, conv_weight, gain):
    rows, width = tokens.shape
    taps = conv_weight.shape[0]
    peers = 8
    group = width // peers
    step = 16
    lanes = 512
    pad = edge.shape[0]

    def body(at_ref, tok, edg, cw, gn, *rest):
        outs, (ext, conv) = rest[:peers], rest[peers:]
        i = pl.program_id(0)

        @pl.when(i == 0)
        def _():
            ext[:pad] = edg[...].astype(F32)

        @pl.when(i > 0)
        def _():
            ext[:pad] = ext[step : step + pad]

        ext[pad:] = tok[...].astype(F32)
        squares = jnp.zeros((step, 128), F32)
        for p in range(width // lanes):
            at = slice(p * lanes, (p + 1) * lanes)
            acc = cw[0:1, at] * ext[pad : pad + step, at]
            for k in range(1, taps):
                acc = acc + cw[k : k + 1, at] * ext[pad - k : pad - k + step, at]
            conv[:, at] = acc
            for j in range(lanes // 128):
                piece = acc[:, j * 128 : (j + 1) * 128]
                squares = squares + piece * piece
        mean = jnp.sum(squares, axis=1, keepdims=True) * (1.0 / width)
        scale = lax.rsqrt(mean + 1e-05)
        for p in range(peers):
            dx, dz = p // 4, p % 4
            peer = (at_ref[1] + dx) % 2 * 4 + (at_ref[2] + dz) % 4
            at = pl.ds(pl.multiple_of(peer * group, group), group)
            outs[p][...] = (conv[:, at] * scale * gn[:, at]).astype(BF16)

    return pl.pallas_call(
        body,
        grid_spec=pltpu.PrefetchScalarGridSpec(
            num_scalar_prefetch=1,
            grid=(rows // step,),
            in_specs=[
                pl.BlockSpec((step, width), lambda i, s: (i, 0)),
                pl.BlockSpec((pad, width), lambda i, s: (0, 0)),
                pl.BlockSpec((taps, width), lambda i, s: (0, 0)),
                pl.BlockSpec((1, width), lambda i, s: (0, 0)),
            ],
            out_specs=[pl.BlockSpec((step, group), lambda i, s: (i, 0))] * peers,
            scratch_shapes=[pltpu.VMEM((pad + step, width), F32), pltpu.VMEM((step, width), F32)],
        ),
        out_shape=[jax.ShapeDtypeStruct((rows, group), BF16)] * peers,
        compiler_params=pltpu.CompilerParams(dimension_semantics=("arbitrary",), vmem_limit_bytes=12 * 2**20),
        cost_estimate=pl.CostEstimate(flops=4000000000, bytes_accessed=4 * rows * width, transcendentals=0),
        name="conv_norm",
    )(place, tokens, edge, conv_weight, gain)


def gate_up(place, near, far, own_gate, other_gate, own_up, other_up):
    per, depth = near.shape
    half, cols = own_gate.shape
    tile = 256
    first = 3

    def body(at_ref, near_ref, far_ref, g0, g1, u0, u1, one, two_near, two_far):
        c = at_ref[0]
        mine = pl.ds(pl.multiple_of(c * half, half), half)
        theirs = pl.ds(pl.multiple_of((1 - c) * half, half), half)

        def product(n, own, other):
            at = pl.ds(pl.multiple_of(n * tile, tile), tile)
            x_mine = jnp.concatenate([near_ref[:, mine], far_ref[:, mine]], 0)
            x_theirs = jnp.concatenate([near_ref[:, theirs], far_ref[:, theirs]], 0)
            total = jnp.dot(x_mine, own[:, at], preferred_element_type=F32) + jnp.dot(
                x_theirs, other[:, at], preferred_element_type=F32
            )
            return total.astype(BF16)

        def to_one(n, _):
            at = pl.ds(pl.multiple_of(n * tile, tile), tile)
            for k, (a, b) in enumerate(((g0, g1), (u0, u1))):
                total = product(n, a, b)
                one[0, k, :, at] = total[:per]
                one[1, k, :, at] = total[per:]
            return 0

        def to_two(n, _):
            at = pl.ds(pl.multiple_of(n * tile, tile), tile)
            for k, (a, b) in enumerate(((g0, g1), (u0, u1))):
                total = product(n + first, a, b)
                two_near[k, :, at] = total[:per]
                two_far[k, :, at] = total[per:]
            return 0

        lax.fori_loop(0, first, to_one, 0)
        lax.fori_loop(0, cols // tile - first, to_two, 0)

    vmem = pl.BlockSpec(memory_space=pltpu.VMEM)
    two_shape = jax.ShapeDtypeStruct((2, per, cols - first * tile), BF16)
    return pl.pallas_call(
        body,
        in_specs=[pl.BlockSpec(memory_space=pltpu.SMEM)] + [vmem] * 6,
        out_specs=[vmem] * 3,
        out_shape=[jax.ShapeDtypeStruct((2, 2, per, first * tile), BF16), two_shape, two_shape],
        compiler_params=pltpu.CompilerParams(vmem_limit_bytes=24 * 2**20),
        cost_estimate=pl.CostEstimate(
            flops=8 * per * depth * cols, bytes_accessed=8 * half * cols, transcendentals=0
        ),
        name="gate_up",
    )(place, near, far, own_gate, other_gate, own_up, other_up)


def down(place, step, near, far, own, other, parts, terms):
    per, depth = near.shape
    half = own.shape[1]
    sub = per // parts

    def body(at_ref, h0, h1, d0, d1, *rest):
        out = rest[-1]
        c = at_ref[0]
        g = pl.program_id(0)

        def write(h):
            for at, w in ((c, d0), (1 - c, d1)):
                total = jnp.dot(h[...], w[...], preferred_element_type=F32).astype(BF16)
                out[:, 0, :, pl.ds(pl.multiple_of(at * half, half), half)] = total.reshape(parts, sub, half)

        @pl.when(g == 0)
        def _():
            write(h0)

        @pl.when(g == 1)
        def _():
            write(h1)

    def block(g, s):
        return (0, (s[1] + g) % 2 * 4 + (s[2] + step) % 4, 0, 0)

    rows = weight = pl.BlockSpec(memory_space=pltpu.VMEM)
    carried = [] if terms is None else [terms]
    return pl.pallas_call(
        body,
        grid_spec=pltpu.PrefetchScalarGridSpec(
            num_scalar_prefetch=1,
            grid=(2,),
            in_specs=[rows, rows, weight, weight] + [pl.BlockSpec(memory_space=pl.ANY)] * len(carried),
            out_specs=pl.BlockSpec((parts, 1, sub, 2 * half), block),
        ),
        out_shape=jax.ShapeDtypeStruct((parts, 8, sub, 2 * half), BF16),
        input_output_aliases={5: 0} if carried else {},
        compiler_params=pltpu.CompilerParams(dimension_semantics=("arbitrary",), vmem_limit_bytes=12 * 2**20),
        cost_estimate=pl.CostEstimate(flops=8 * per * depth * half, bytes_accessed=4 * depth * half, transcendentals=0),
        name="down",
    )(place, near, far, own, other, *carried)


def total(*terms):
    out = terms[0].astype(F32)
    for t in terms[1:]:
        out = out + t.astype(F32)
    return out


def swiglu(both):
    return (jax.nn.silu(both[0]) * both[1]).astype(BF16)


def shards(tokens, conv_weight, norm_gain, gate_weight, up_weight, down_weight):
    parts = lax.axis_size(TP)
    seq = lax.axis_size(SEQ)
    place = jnp.stack([lax.axis_index(a).astype(jnp.int32) for a in ("c", "xh", "z")])
    swap = lambda w: lax.ppermute(w, "c", [(0, 1), (1, 0)])
    edge = lax.ppermute(tokens[-8:], SEQ, [(i, i + 1) for i in range(seq - 1)])
    gate_other = swap(gate_weight)
    up_other = swap(up_weight)
    down_other = swap(down_weight)
    normed = conv_norm(place, tokens, edge, conv_weight, norm_gain[None, :])
    rows = {(0, 0): normed[0]}
    for dx, dz in PEERS:
        rows[dx, -dz % 4] = hop(normed[dx * 4 + dz], dx, dz)
    one, near, far, one_in, far_in = {}, {}, {}, {}, {}
    for e in STEPS:
        one[e], near[e], far[e] = gate_up(place, rows[0, e], rows[1, e], gate_weight, gate_other, up_weight, up_other)
        far_in[e] = hop(far[e], 1, 0)
        if e:
            one_in[e] = hop(one[e], 0, e)
    two_in = {}
    for e in STEPS[1:]:
        both = total(near[e], far_in[e]).astype(BF16)
        two_in[e] = hop(both, 0, e)
    firsts = [one[0]] + [one_in[e] for e in STEPS[1:]]
    across = total(*[f[1] for f in firsts]).astype(BF16)
    last = hop(across, 1, 0)
    left = total(*[f[0] for f in firsts], last)
    right = total(near[0], far_in[0], *[two_in[e] for e in STEPS[1:]])
    hidden = jnp.concatenate([swiglu(left), swiglu(right)], 1)
    blocks = {(0, 0): hidden}
    for dx, dz in PEERS:
        blocks[dx, -dz % 4] = hop(hidden, dx, dz)
    terms = None
    for e in STEPS:
        terms = down(place, e, blocks[0, e], blocks[1, e], down_weight, down_other, parts, terms)
    arrived = lax.all_to_all(terms, TP, split_axis=0, concat_axis=0, tiled=True)
    summed = arrived.astype(F32).sum(axis=0).astype(BF16)
    out = lax.all_to_all(summed, CHIPS, split_axis=0, concat_axis=0, tiled=True)
    return jnp.transpose(out, (1, 0, 2)).reshape(out.shape[1], -1)


def solution(mesh):
    fine = Mesh(np.asarray(mesh.devices).reshape(*SHAPE.values()), tuple(SHAPE))
    in_specs = (P(SEQ, None), P(), P(), P(SEQ, TP), P(SEQ, TP), P(TP, SEQ))
    out_specs = P(SEQ + TP, None)
    return jax.shard_map(shards, mesh=fine, in_specs=in_specs, out_specs=out_specs, check_vma=False)
```

time: 305 us -> 212 us (0.70)
  the two profiles are of different devices: /device:TPU:1 before, /device:TPU:0 now
where the time goes in v2:
time: 212 us
  waiting for transfers between devices  74 us (35%)
  starting transfers between devices  56 us (26%)
  blocking collectives  42.8 us (20%)
  Pallas kernels  31.4 us (15%)
  local copies, waits for them, and re-layouts  4.9 us (2%)
  other arithmetic  2.19 us (1%)
    ppermute x25, waiting for transfers between devices, hop(): return lax.ppermute(x, CHIPS, pairs)  71 us
    ppermute x25, starting transfers between devices, hop(): return lax.ppermute(x, CHIPS, pairs)  53.5 us
    all_to_all x1, blocking collectives, shards(): arrived = lax.all_to_all(terms, TP, split_axis=0, concat_axis=0, tiled=True)  28.5 us
    pallas_call x4, Pallas kernels, gate_up(): pl.pallas_call(body, in_specs=[pl.BlockSpec(memory_space=pltpu.SMEM)] + [...  18.5 us
    all_to_all x1, blocking collectives, shards(): out = lax.all_to_all(summed, CHIPS, split_axis=0, concat_axis=0, tiled=True)  14.3 us
    pallas_call x4, Pallas kernels, down(): pl.pallas_call(body, grid_spec=pltpu.PrefetchScalarGridSpec(num_scalar_pr...  7.88 us
    pallas_call x1, Pallas kernels, conv_norm(): pl.pallas_call(body, grid_spec=pltpu.PrefetchScalarGridSpec(num_scalar_pr...  5.03 us
  transfers between devices with their start and end apart: 29, of which 13 were waited for; matrix products, arithmetic and copies ran while one was open for 1% of the time, Pallas kernels for 14%

profile of v2, /device:TPU:0, one launch (start us, length us, event | category | flops | bytes accessed | tf_op | source)
XLA Modules:
  0.0 211.7 jit_solution(8656328248889988009)
XLA Ops:
  0.5 0.9 slice.39
  1.4 1.9 collective-permute-start
  3.4 3.0 %collective-permute-done.edg = bf16[8,8192]{1,0:T(8,128)(2,1)S(1)} collective-permute-done((bf16[8,8192]{1,0:T(8,128)(2,1)S(1)}, bf16[8,8192]{1,0:T(8,128)(2,1)S(1)}, u32[]{:S(2)}, u32[]{:S(2)}) %collective-permute-start) | collective-permute-done | bytes 131104 | tf_op jit(solution)/shard_map/ppermute | solution.py:202
  6.4 1.6 copy-done.3
  8.0 0.9 copy-done.4
  8.9 0.8 copy-done.5
  9.7 5.0 %conv_norm.1 = (bf16[128,1024]{1,0:T(8,128)(2,1)S(1)}, bf16[128,1024]{1,0:T(8,128)(2,1)S(1)}, bf16[128,1024]{1,0:T(8,128)(2,1)S(1)}, bf16[128,1024]{1,0:T(8,128)...) custom-call(s32[3]{0:T(128)S(1)} %pad_add_fusion.at_ref, ...), custom_call_target="tpu_custom_call" | custom-call | flops 4000000000 | bytes 4194304 | tf_op jit(solution)/shard_map/conv_norm/pallas_call | solution.py:67
  14.7 5.3 %collective-permute-start.10 = (bf16[128,1024]{1,0:T(8,128)(2,1)S(1)}, bf16[128,1024]{1,0:T(8,128)(2,1)S(1)}, u32[]{:S(2)}, u32[]{:S(2)}) collective-permute-start(bf16[128,1024]{1,0:T(8,128)(2,1)S(1)} %get-tuple-element.34), channel_id=1, source_target_pairs={{0,32},{16,48},{32,0},{48,16},{64,96},{80,112},{96,64},{112,80},{1... | collective-permute-start | bytes 786440 | tf_op jit(solution)/shard_map/ppermute | solution.py:24
  20.1 5.7 %collective-permute-start.11 = (bf16[128,1024]{1,0:T(8,128)(2,1)S(1)}, bf16[128,1024]{1,0:T(8,128)(2,1)S(1)}, u32[]{:S(2)}, u32[]{:S(2)}) collective-permute-start(bf16[128,1024]{1,0:T(8,128)(2,1)S(1)} %get-tuple-element.35), channel_id=1, source_target_pairs={{0,96},{16,112},{32,64},{48,80},{64,32},{80,48},{96,0},{112,16},{1... | collective-permute-start | bytes 786440 | tf_op jit(solution)/shard_map/ppermute | solution.py:24
  25.8 6.6 %collective-permute-done.10.near_ref = bf16[128,1024]{1,0:T(8,128)(2,1)S(1)} collective-permute-done((bf16[128,1024]{1,0:T(8,128)(2,1)S(1)}, bf16[128,1024]{1,0:T(8,128)(2,1)S(1)}, u32[]{:S(2)}, u32[]{:S(2)}) %collective-permute-start.10) | collective-permute-done | bytes 262176 | tf_op jit(solution)/shard_map/ppermute | solution.py:24
  32.4 3.1 %collective-permute-start.8 = (bf16[128,1024]{1,0:T(8,128)(2,1)S(1)}, bf16[128,1024]{1,0:T(8,128)(2,1)S(1)}, u32[]{:S(2)}, u32[]{:S(2)}) collective-permute-start(bf16[128,1024]{1,0:T(8,128)(2,1)S(1)} %get-tuple-element.32), channel_id=1, source_target_pairs={{0,80},{16,96},{32,112},{48,64},{64,16},{80,32},{96,48},{112,0},{1... | collective-permute-start | bytes 786440 | tf_op jit(solution)/shard_map/ppermute | solution.py:24
  35.5 6.8 %collective-permute-start.4 = (bf16[128,1024]{1,0:T(8,128)(2,1)S(1)}, bf16[128,1024]{1,0:T(8,128)(2,1)S(1)}, u32[]{:S(2)}, u32[]{:S(2)}) collective-permute-start(bf16[128,1024]{1,0:T(8,128)(2,1)S(1)} %get-tuple-element.28), channel_id=1, source_target_pairs={{0,48},{16,0},{32,16},{48,32},{64,112},{80,64},{96,80},{112,96},{1... | collective-permute-start | bytes 786440 | tf_op jit(solution)/shard_map/ppermute | solution.py:24
  42.3 3.0 %collective-permute-start.1 = (bf16[128,1024]{1,0:T(8,128)(2,1)S(1)}, bf16[128,1024]{1,0:T(8,128)(2,1)S(1)}, u32[]{:S(2)}, u32[]{:S(2)}) collective-permute-start(bf16[128,1024]{1,0:T(8,128)(2,1)S(1)} %get-tuple-element.26), channel_id=1, source_target_pairs={{0,64},{16,80},{32,96},{48,112},{64,0},{80,16},{96,32},{112,48},{1... | collective-permute-start | bytes 786440 | tf_op jit(solution)/shard_map/ppermute | solution.py:24
  45.4 4.6 %gate_up.7 = (bf16[2,2,128,768]{3,2,1,0:T(8,128)(2,1)S(1)}, bf16[2,128,1024]{2,1,0:T(8,128)(2,1)S(1)}, bf16[2,128,1024]{2,1,0:T(8,128)(2,1)S(1)}) custom-call(s32[3]{0:T(128)S(1)} %pad_add_fusion.at_ref, bf16[128,1024]{1,0:T(8,128)(2,1)S(1)} %collective-permute-done.10.near_ref, bf16[128,1024]{1,0:T(8,128)(2,1)S(1)} %collective-permute-done.11.far_ref, ...), custom_call_target="tpu_custom_call" | custom-call | flops 1879048192 | bytes 7340032 | tf_op jit(solution)/shard_map/gate_up/pallas_call | solution.py:129
  50.7 4.6 %gate_up.6 = (bf16[2,2,128,768]{3,2,1,0:T(8,128)(2,1)S(1)}, bf16[2,128,1024]{2,1,0:T(8,128)(2,1)S(1)}, bf16[2,128,1024]{2,1,0:T(8,128)(2,1)S(1)}) custom-call(s32[3]{0:T(128)S(1)} %pad_add_fusion.at_ref, bf16[128,1024]{1,0:T(8,128)(2,1)S(1)} %collective-permute-done.7.near_ref, bf16[128,1024]{1,0:T(8,128)(2,1)S(1)} %collective-permute-done.8.far_ref, ...), custom_call_target="tpu_custom_call" | custom-call | flops 1879048192 | bytes 7340032 | tf_op jit(solution)/shard_map/gate_up/pallas_call | solution.py:129
  55.3 3.0 %collective-permute-start.17 = (bf16[2,128,1024]{2,1,0:T(8,128)(2,1)S(1)}, bf16[2,128,1024]{2,1,0:T(8,128)(2,1)S(1)}, u32[]{:S(2)}, u32[]{:S(2)}) collective-permute-start(bf16[2,128,1024]{2,1,0:T(8,128)(2,1)S(1)} %get-tuple-element.42), channel_id=1, source_target_pairs={{0,64},{16,80},{32,96},{48,112},{64,0},{80,16},{96,32},{112,48},{1... | collective-permute-start | bytes 1572872 | tf_op jit(solution)/shard_map/ppermute | solution.py:24
  58.4 4.6 %gate_up.5 = (bf16[2,2,128,768]{3,2,1,0:T(8,128)(2,1)S(1)}, bf16[2,128,1024]{2,1,0:T(8,128)(2,1)S(1)}, bf16[2,128,1024]{2,1,0:T(8,128)(2,1)S(1)}) custom-call(s32[3]{0:T(128)S(1)} %pad_add_fusion.at_ref, bf16[128,1024]{1,0:T(8,128)(2,1)S(1)} %collective-permute-done.4.near_ref, bf16[128,1024]{1,0:T(8,128)(2,1)S(1)} %collective-permute-done.5.far_ref, ...), custom_call_target="tpu_custom_call" | custom-call | flops 1879048192 | bytes 7340032 | tf_op jit(solution)/shard_map/gate_up/pallas_call | solution.py:129
  63.7 1.4 collective-permute-start.12
  65.1 2.7 %collective-permute-start.9 = (bf16[2,2,128,768]{3,2,1,0:T(8,128)(2,1)S(1)}, bf16[2,2,128,768]{3,2,1,0:T(8,128)(2,1)S(1)}, u32[]{:S(2)}, u32[]{:S(2)}) collective-permute-start(bf16[2,2,128,768]{3,2,1,0:T(8,128)(2,1)S(1)} %get-tuple-element.33), channel_id=1, source_target_pairs={{0,48},{16,0},{32,16},{48,32},{64,112},{80,64},{96,80},{112,96},{1... | collective-permute-start | bytes 2359304 | tf_op jit(solution)/shard_map/ppermute | solution.py:24
  67.8 4.6 %gate_up.4 = (bf16[2,2,128,768]{3,2,1,0:T(8,128)(2,1)S(1)}, bf16[2,128,1024]{2,1,0:T(8,128)(2,1)S(1)}, bf16[2,128,1024]{2,1,0:T(8,128)(2,1)S(1)}) custom-call(s32[3]{0:T(128)S(1)} %pad_add_fusion.at_ref, bf16[128,1024]{1,0:T(8,128)(2,1)S(1)} %get-tuple-element.25.near_ref, bf16[128,1024]{1,0:T(8,128)(2,1)S(1)} %collective-permute-done.1.far_ref, ...), custom_call_target="tpu_custom_call" | custom-call | flops 1879048192 | bytes 7340032 | tf_op jit(solution)/shard_map/gate_up/pallas_call | solution.py:129
  72.7 7.9 %collective-permute-done.17 = bf16[2,128,1024]{2,1,0:T(8,128)(2,1)S(1)} collective-permute-done((bf16[2,128,1024]{2,1,0:T(8,128)(2,1)S(1)}, bf16[2,128,1024]{2,1,0:T(8,128)(2,1)S(1)}, u32[]{:S(2)}, u32[]{:S(2)}) %collective-permute-start.17) | collective-permute-done | bytes 524320 | tf_op jit(solution)/shard_map/ppermute | solution.py:24
  81.3 10.5 %collective-permute-done.15 = bf16[2,128,1024]{2,1,0:T(8,128)(2,1)S(1)} collective-permute-done((bf16[2,128,1024]{2,1,0:T(8,128)(2,1)S(1)}, bf16[2,128,1024]{2,1,0:T(8,128)(2,1)S(1)}, u32[]{:S(2)}, u32[]{:S(2)}) %collective-permute-start.15) | collective-permute-done | bytes 524320 | tf_op jit(solution)/shard_map/ppermute | solution.py:24
  91.8 2.5 %collective-permute-start.20 = (bf16[2,128,1024]{2,1,0:T(8,128)(2,1)S(1)}, bf16[2,128,1024]{2,1,0:T(8,128)(2,1)S(1)}, u32[]{:S(2)}, u32[]{:S(2)}) collective-permute-start(bf16[2,128,1024]{2,1,0:T(8,128)(2,1)S(1)} %add_convert_fusion), channel_id=1, source_target_pairs={{0,32},{16,48},{32,0},{48,16},{64,96},{80,112},{96,64},{112,80},{1... | collective-permute-start | bytes 1572872 | tf_op jit(solution)/shard_map/ppermute | solution.py:24
  94.6 1.3 collective-permute-start.18
  95.8 5.3 %collective-permute-done.9 = bf16[2,2,128,768]{3,2,1,0:T(8,128)(2,1)S(1)} collective-permute-done((bf16[2,2,128,768]{3,2,1,0:T(8,128)(2,1)S(1)}, bf16[2,2,128,768]{3,2,1,0:T(8,128)(2,1)S(1)}, u32[]{:S(2)}, u32[]{:S(2)}) %collective-permute-start.9) | collective-permute-done | bytes 786464 | tf_op jit(solution)/shard_map/ppermute | solution.py:24
  101.5 3.9 %collective-permute-start.13 = (bf16[2,128,768]{2,1,0:T(8,128)(2,1)S(1)}, bf16[2,128,768]{2,1,0:T(8,128)(2,1)S(1)}, u32[]{:S(2)}, u32[]{:S(2)}) collective-permute-start(bf16[2,128,768]{2,1,0:T(8,128)(2,1)S(1)} %fusion.2), channel_id=1, source_target_pairs={{0,64},{16,80},{32,96},{48,112},{64,0},{80,16},{96,32},{112,48},{1... | collective-permute-start | bytes 1179656 | tf_op jit(solution)/shard_map/ppermute | solution.py:24
  105.4 5.4 %collective-permute-done.20 = bf16[2,128,1024]{2,1,0:T(8,128)(2,1)S(1)} collective-permute-done((bf16[2,128,1024]{2,1,0:T(8,128)(2,1)S(1)}, bf16[2,128,1024]{2,1,0:T(8,128)(2,1)S(1)}, u32[]{:S(2)}, u32[]{:S(2)}) %collective-permute-start.20) | collective-permute-done | bytes 524320 | tf_op jit(solution)/shard_map/ppermute | solution.py:24
  110.8 4.4 %collective-permute-done.18 = bf16[2,128,1024]{2,1,0:T(8,128)(2,1)S(1)} collective-permute-done((bf16[2,128,1024]{2,1,0:T(8,128)(2,1)S(1)}, bf16[2,128,1024]{2,1,0:T(8,128)(2,1)S(1)}, u32[]{:S(2)}, u32[]{:S(2)}) %collective-permute-start.18) | collective-permute-done | bytes 524320 | tf_op jit(solution)/shard_map/ppermute | solution.py:24
  115.2 2.2 %collective-permute-done.16 = bf16[2,128,1024]{2,1,0:T(8,128)(2,1)S(1)} collective-permute-done((bf16[2,128,1024]{2,1,0:T(8,128)(2,1)S(1)}, bf16[2,128,1024]{2,1,0:T(8,128)(2,1)S(1)}, u32[]{:S(2)}, u32[]{:S(2)}) %collective-permute-start.16) | collective-permute-done | bytes 524320 | tf_op jit(solution)/shard_map/ppermute | solution.py:24
  118.4 0.7 collective-permute-start.26
  119.1 2.5 %collective-permute-start.28 = (bf16[128,1792]{1,0:T(8,128)(2,1)S(1)}, bf16[128,1792]{1,0:T(8,128)(2,1)S(1)}, u32[]{:S(2)}, u32[]{:S(2)}) collective-permute-start(bf16[128,1792]{1,0:T(8,128)(2,1)S(1)} %pad_maximum_fusion.h0), channel_id=1, source_target_pairs={{0,64},{16,80},{32,96},{48,112},{64,0},{80,16},{96,32},{112,48},{1... | collective-permute-start | bytes 1376264 | tf_op jit(solution)/shard_map/ppermute | solution.py:24
  121.6 1.6 collective-permute-start.27
  123.3 0.9 collective-permute-start.24
  124.1 3.4 %collective-permute-start.25 = (bf16[128,1792]{1,0:T(8,128)(2,1)S(1)}, bf16[128,1792]{1,0:T(8,128)(2,1)S(1)}, u32[]{:S(2)}, u32[]{:S(2)}) collective-permute-start(bf16[128,1792]{1,0:T(8,128)(2,1)S(1)} %pad_maximum_fusion.h0), channel_id=1, source_target_pairs={{0,80},{16,96},{32,112},{48,64},{64,16},{80,32},{96,48},{112,0},{1... | collective-permute-start | bytes 1376264 | tf_op jit(solution)/shard_map/ppermute | solution.py:24
  127.5 1.6 collective-permute-done.26.h0
  129.1 1.4 collective-permute-start.21
  130.5 3.5 %collective-permute-done.28.h1 = bf16[128,1792]{1,0:T(8,128)(2,1)S(1)} collective-permute-done((bf16[128,1792]{1,0:T(8,128)(2,1)S(1)}, bf16[128,1792]{1,0:T(8,128)(2,1)S(1)}, u32[]{:S(2)}, u32[]{:S(2)}) %collective-permute-start.28) | collective-permute-done | bytes 458784 | tf_op jit(solution)/shard_map/ppermute | solution.py:24
  134.0 2.3 %collective-permute-start.22 = (bf16[128,1792]{1,0:T(8,128)(2,1)S(1)}, bf16[128,1792]{1,0:T(8,128)(2,1)S(1)}, u32[]{:S(2)}, u32[]{:S(2)}) collective-permute-start(bf16[128,1792]{1,0:T(8,128)(2,1)S(1)} %pad_maximum_fusion.h0), channel_id=1, source_target_pairs={{0,96},{16,112},{32,64},{48,80},{64,32},{80,48},{96,0},{112,16},{1... | collective-permute-start | bytes 1376264 | tf_op jit(solution)/shard_map/ppermute | solution.py:24
  136.3 2.0 down.4.rest_0_
  138.3 6.4 %collective-permute-done.27.h1 = bf16[128,1792]{1,0:T(8,128)(2,1)S(1)} collective-permute-done((bf16[128,1792]{1,0:T(8,128)(2,1)S(1)}, bf16[128,1792]{1,0:T(8,128)(2,1)S(1)}, u32[]{:S(2)}, u32[]{:S(2)}) %collective-permute-start.27) | collective-permute-done | bytes 458784 | tf_op jit(solution)/shard_map/ppermute | solution.py:24
  144.7 2.0 down.5.rest_0_
  146.7 9.1 %collective-permute-done.25.h1 = bf16[128,1792]{1,0:T(8,128)(2,1)S(1)} collective-permute-done((bf16[128,1792]{1,0:T(8,128)(2,1)S(1)}, bf16[128,1792]{1,0:T(8,128)(2,1)S(1)}, u32[]{:S(2)}, u32[]{:S(2)}) %collective-permute-start.25) | collective-permute-done | bytes 458784 | tf_op jit(solution)/shard_map/ppermute | solution.py:24
  155.8 2.0 down.6.rest_0_
  157.8 8.0 %collective-permute-done.21.h0 = bf16[128,1792]{1,0:T(8,128)(2,1)S(1)} collective-permute-done((bf16[128,1792]{1,0:T(8,128)(2,1)S(1)}, bf16[128,1792]{1,0:T(8,128)(2,1)S(1)}, u32[]{:S(2)}, u32[]{:S(2)}) %collective-permute-start.21) | collective-permute-done | bytes 458784 | tf_op jit(solution)/shard_map/ppermute | solution.py:24
  165.8 2.0 down.7
  167.8 28.5 %all_to_all.10 = bf16[8,8,16,1024]{3,2,1,0:T(8,128)(2,1)S(1)} all-to-all(bf16[8,8,16,1024]{3,2,1,0:T(8,128)(2,1)S(1)} %down.7), channel_id=1, replica_groups=mesh['xh'=2,'z'=4,'c'=2,'y'=4,'xl'=2] {'y','xl'}, dimensions={0} | all-to-all | bytes 4194304 | tf_op jit(solution)/shard_map/all_to_all | solution.py:232
  196.6 14.3 %all_to_all.11 = bf16[8,16,1024]{2,1,0:T(8,128)(2,1)S(1)} all-to-all(bf16[8,16,1024]{2,1,0:T(8,128)(2,1)S(1)} %reduce_sum.12), channel_id=1, replica_groups=mesh['xh'=2,'z'=4,'c'=2,'y'=4,'xl'=2] {'xh','z'}, dimensions={0} | all-to-all | bytes 524288 | tf_op jit(solution)/shard_map/all_to_all | solution.py:234
  211.0 0.7 copy.11
  (46 shorter events, 4.7 us)
Async XLA Ops:
  0.0 42.3 %collective-permute-start.2 = (bf16[512,1792]{1,0:T(8,128)(2,1)}, bf16[512,1792]{1,0:T(8,128)(2,1)S(1)}, u32[]{:S(2)}, u32[]{:S(2)}) collective-permute-start(bf16[512,1792]{1,0:T(8,128)(2,1)} %g0.7), channel_id=1, source_target_pairs={{0,8},{8,0},{1,9},{9,1},{2,10},{10,2},{3,11},{11,3},{4,12},{12,4},... | collective-permute-start | bytes 5505032 | tf_op jit(solution)/shard_map/ppermute | solution.py:201
  0.0 42.3 %collective-permute-start.3 = (bf16[512,1792]{1,0:T(8,128)(2,1)}, bf16[512,1792]{1,0:T(8,128)(2,1)}, u32[]{:S(2)}, u32[]{:S(2)}) collective-permute-start(bf16[512,1792]{1,0:T(8,128)(2,1)} %u0.7), channel_id=1, source_target_pairs={{0,8},{8,0},{1,9},{9,1},{2,10},{10,2},{3,11},{11,3},{4,12},{12,4},... | collective-permute-start | bytes 5505032 | tf_op jit(solution)/shard_map/ppermute | solution.py:201
  1.4 5.0 %collective-permute-start = (bf16[8,8192]{1,0:T(8,128)(2,1)S(1)}, bf16[8,8192]{1,0:T(8,128)(2,1)S(1)}, u32[]{:S(2)}, u32[]{:S(2)}) collective-permute-start(bf16[8,8192]{1,0:T(8,128)(2,1)S(1)} %slice.39), channel_id=1, source_target_pairs={{0,8},{8,16},{16,24},{24,32},{32,40},{40,48},{48,56},{56,64},{64,7... | collective-permute-start | bytes 393224 | tf_op jit(solution)/shard_map/ppermute | solution.py:202
  6.4 1.6 copy-start.3
  8.0 0.9 copy-start.4
  8.9 0.8 copy-start.5
  9.7 35.7 %copy-start.1 = (bf16[512,1792]{1,0:T(8,128)(2,1)S(1)}, bf16[512,1792]{1,0:T(8,128)(2,1)}, u32[]{:S(2)}) copy-start(bf16[512,1792]{1,0:T(8,128)(2,1)} %g0.7) | copy-start | bytes 5505028
  9.7 35.7 %copy-start.2 = (bf16[512,1792]{1,0:T(8,128)(2,1)S(1)}, bf16[512,1792]{1,0:T(8,128)(2,1)}, u32[]{:S(2)}) copy-start(bf16[512,1792]{1,0:T(8,128)(2,1)} %u0.7) | copy-start | bytes 5505028
  14.7 17.7 %collective-permute-start.10 = (bf16[128,1024]{1,0:T(8,128)(2,1)S(1)}, bf16[128,1024]{1,0:T(8,128)(2,1)S(1)}, u32[]{:S(2)}, u32[]{:S(2)}) collective-permute-start(bf16[128,1024]{1,0:T(8,128)(2,1)S(1)} %get-tuple-element.34), channel_id=1, source_target_pairs={{0,32},{16,48},{32,0},{48,16},{64,96},{80,112},{96,64},{112,80},{1... | collective-permute-start | bytes 786440 | tf_op jit(solution)/shard_map/ppermute | solution.py:24
  20.1 15.4 %collective-permute-start.11 = (bf16[128,1024]{1,0:T(8,128)(2,1)S(1)}, bf16[128,1024]{1,0:T(8,128)(2,1)S(1)}, u32[]{:S(2)}, u32[]{:S(2)}) collective-permute-start(bf16[128,1024]{1,0:T(8,128)(2,1)S(1)} %get-tuple-element.35), channel_id=1, source_target_pairs={{0,96},{16,112},{32,64},{48,80},{64,32},{80,48},{96,0},{112,16},{1... | collective-permute-start | bytes 786440 | tf_op jit(solution)/shard_map/ppermute | solution.py:24
  25.8 24.2 %collective-permute-start.7 = (bf16[128,1024]{1,0:T(8,128)(2,1)S(1)}, bf16[128,1024]{1,0:T(8,128)(2,1)S(1)}, u32[]{:S(2)}, u32[]{:S(2)}) collective-permute-start(bf16[128,1024]{1,0:T(8,128)(2,1)S(1)} %get-tuple-element.31), channel_id=1, source_target_pairs={{0,16},{16,32},{32,48},{48,0},{64,80},{80,96},{96,112},{112,64},{1... | collective-permute-start | bytes 786440 | tf_op jit(solution)/shard_map/ppermute | solution.py:24
  32.4 18.2 %collective-permute-start.8 = (bf16[128,1024]{1,0:T(8,128)(2,1)S(1)}, bf16[128,1024]{1,0:T(8,128)(2,1)S(1)}, u32[]{:S(2)}, u32[]{:S(2)}) collective-permute-start(bf16[128,1024]{1,0:T(8,128)(2,1)S(1)} %get-tuple-element.32), channel_id=1, source_target_pairs={{0,80},{16,96},{32,112},{48,64},{64,16},{80,32},{96,48},{112,0},{1... | collective-permute-start | bytes 786440 | tf_op jit(solution)/shard_map/ppermute | solution.py:24
  35.5 22.9 %collective-permute-start.4 = (bf16[128,1024]{1,0:T(8,128)(2,1)S(1)}, bf16[128,1024]{1,0:T(8,128)(2,1)S(1)}, u32[]{:S(2)}, u32[]{:S(2)}) collective-permute-start(bf16[128,1024]{1,0:T(8,128)(2,1)S(1)} %get-tuple-element.28), channel_id=1, source_target_pairs={{0,48},{16,0},{32,16},{48,32},{64,112},{80,64},{96,80},{112,96},{1... | collective-permute-start | bytes 786440 | tf_op jit(solution)/shard_map/ppermute | solution.py:24
  42.3 16.0 %collective-permute-start.5 = (bf16[128,1024]{1,0:T(8,128)(2,1)S(1)}, bf16[128,1024]{1,0:T(8,128)(2,1)S(1)}, u32[]{:S(2)}, u32[]{:S(2)}) collective-permute-start(bf16[128,1024]{1,0:T(8,128)(2,1)S(1)} %get-tuple-element.29), channel_id=1, source_target_pairs={{0,112},{16,64},{32,80},{48,96},{64,48},{80,0},{96,16},{112,32},{1... | collective-permute-start | bytes 786440 | tf_op jit(solution)/shard_map/ppermute | solution.py:24
  42.3 22.7 %collective-permute-start.1 = (bf16[128,1024]{1,0:T(8,128)(2,1)S(1)}, bf16[128,1024]{1,0:T(8,128)(2,1)S(1)}, u32[]{:S(2)}, u32[]{:S(2)}) collective-permute-start(bf16[128,1024]{1,0:T(8,128)(2,1)S(1)} %get-tuple-element.26), channel_id=1, source_target_pairs={{0,64},{16,80},{32,96},{48,112},{64,0},{80,16},{96,32},{112,48},{1... | collective-permute-start | bytes 786440 | tf_op jit(solution)/shard_map/ppermute | solution.py:24
  50.0 22.4 %collective-permute-start.19 = (bf16[2,128,1024]{2,1,0:T(8,128)(2,1)S(1)}, bf16[2,128,1024]{2,1,0:T(8,128)(2,1)S(1)}, u32[]{:S(2)}, u32[]{:S(2)}) collective-permute-start(bf16[2,128,1024]{2,1,0:T(8,128)(2,1)S(1)} %get-tuple-element.44), channel_id=1, source_target_pairs={{0,64},{16,80},{32,96},{48,112},{64,0},{80,16},{96,32},{112,48},{1... | collective-permute-start | bytes 1572872 | tf_op jit(solution)/shard_map/ppermute | solution.py:24
  55.3 25.3 %collective-permute-start.17 = (bf16[2,128,1024]{2,1,0:T(8,128)(2,1)S(1)}, bf16[2,128,1024]{2,1,0:T(8,128)(2,1)S(1)}, u32[]{:S(2)}, u32[]{:S(2)}) collective-permute-start(bf16[2,128,1024]{2,1,0:T(8,128)(2,1)S(1)} %get-tuple-element.42), channel_id=1, source_target_pairs={{0,64},{16,80},{32,96},{48,112},{64,0},{80,16},{96,32},{112,48},{1... | collective-permute-start | bytes 1572872 | tf_op jit(solution)/shard_map/ppermute | solution.py:24
  63.0 28.8 %collective-permute-start.15 = (bf16[2,128,1024]{2,1,0:T(8,128)(2,1)S(1)}, bf16[2,128,1024]{2,1,0:T(8,128)(2,1)S(1)}, u32[]{:S(2)}, u32[]{:S(2)}) collective-permute-start(bf16[2,128,1024]{2,1,0:T(8,128)(2,1)S(1)} %get-tuple-element.40), channel_id=1, source_target_pairs={{0,64},{16,80},{32,96},{48,112},{64,0},{80,16},{96,32},{112,48},{1... | collective-permute-start | bytes 1572872 | tf_op jit(solution)/shard_map/ppermute | solution.py:24
  63.7 30.9 %collective-permute-start.12 = (bf16[2,2,128,768]{3,2,1,0:T(8,128)(2,1)S(1)}, bf16[2,2,128,768]{3,2,1,0:T(8,128)(2,1)S(1)}, u32[]{:S(2)}, u32[]{:S(2)}) collective-permute-start(bf16[2,2,128,768]{3,2,1,0:T(8,128)(2,1)S(1)} %get-tuple-element.36), channel_id=1, source_target_pairs={{0,32},{16,48},{32,0},{48,16},{64,96},{80,112},{96,64},{112,80},{1... | collective-permute-start | bytes 2359304 | tf_op jit(solution)/shard_map/ppermute | solution.py:24
  65.1 36.1 %collective-permute-start.9 = (bf16[2,2,128,768]{3,2,1,0:T(8,128)(2,1)S(1)}, bf16[2,2,128,768]{3,2,1,0:T(8,128)(2,1)S(1)}, u32[]{:S(2)}, u32[]{:S(2)}) collective-permute-start(bf16[2,2,128,768]{3,2,1,0:T(8,128)(2,1)S(1)} %get-tuple-element.33), channel_id=1, source_target_pairs={{0,48},{16,0},{32,16},{48,32},{64,112},{80,64},{96,80},{112,96},{1... | collective-permute-start | bytes 2359304 | tf_op jit(solution)/shard_map/ppermute | solution.py:24
  72.5 28.7 %collective-permute-start.6 = (bf16[2,2,128,768]{3,2,1,0:T(8,128)(2,1)S(1)}, bf16[2,2,128,768]{3,2,1,0:T(8,128)(2,1)S(1)}, u32[]{:S(2)}, u32[]{:S(2)}) collective-permute-start(bf16[2,2,128,768]{3,2,1,0:T(8,128)(2,1)S(1)} %get-tuple-element.30), channel_id=1, source_target_pairs={{0,16},{16,32},{32,48},{48,0},{64,80},{80,96},{96,112},{112,64},{1... | collective-permute-start | bytes 2359304 | tf_op jit(solution)/shard_map/ppermute | solution.py:24
  72.5 28.6 %copy-start = (bf16[1792,512]{1,0:T(8,128)(2,1)S(1)}, bf16[1792,512]{1,0:T(8,128)(2,1)}, u32[]{:S(2)}) copy-start(bf16[1792,512]{1,0:T(8,128)(2,1)} %d0.7) | copy-start | bytes 5505028
  80.6 20.9 %collective-permute-start.14 = (bf16[2,128,1024]{2,1,0:T(8,128)(2,1)S(1)}, bf16[2,128,1024]{2,1,0:T(8,128)(2,1)S(1)}, u32[]{:S(2)}, u32[]{:S(2)}) collective-permute-start(bf16[2,128,1024]{2,1,0:T(8,128)(2,1)S(1)} %get-tuple-element.38), channel_id=1, source_target_pairs={{0,64},{16,80},{32,96},{48,112},{64,0},{80,16},{96,32},{112,48},{1... | collective-permute-start | bytes 1572872 | tf_op jit(solution)/shard_map/ppermute | solution.py:24
  91.8 18.9 %collective-permute-start.20 = (bf16[2,128,1024]{2,1,0:T(8,128)(2,1)S(1)}, bf16[2,128,1024]{2,1,0:T(8,128)(2,1)S(1)}, u32[]{:S(2)}, u32[]{:S(2)}) collective-permute-start(bf16[2,128,1024]{2,1,0:T(8,128)(2,1)S(1)} %add_convert_fusion), channel_id=1, source_target_pairs={{0,32},{16,48},{32,0},{48,16},{64,96},{80,112},{96,64},{112,80},{1... | collective-permute-start | bytes 1572872 | tf_op jit(solution)/shard_map/ppermute | solution.py:24
  94.6 20.6 %collective-permute-start.18 = (bf16[2,128,1024]{2,1,0:T(8,128)(2,1)S(1)}, bf16[2,128,1024]{2,1,0:T(8,128)(2,1)S(1)}, u32[]{:S(2)}, u32[]{:S(2)}) collective-permute-start(bf16[2,128,1024]{2,1,0:T(8,128)(2,1)S(1)} %add_convert_fusion.1), channel_id=1, source_target_pairs={{0,48},{16,0},{32,16},{48,32},{64,112},{80,64},{96,80},{112,96},{1... | collective-permute-start | bytes 1572872 | tf_op jit(solution)/shard_map/ppermute | solution.py:24
  101.2 16.2 %collective-permute-start.16 = (bf16[2,128,1024]{2,1,0:T(8,128)(2,1)S(1)}, bf16[2,128,1024]{2,1,0:T(8,128)(2,1)S(1)}, u32[]{:S(2)}, u32[]{:S(2)}) collective-permute-start(bf16[2,128,1024]{2,1,0:T(8,128)(2,1)S(1)} %add_convert_fusion.2), channel_id=1, source_target_pairs={{0,16},{16,32},{32,48},{48,0},{64,80},{80,96},{96,112},{112,64},{1... | collective-permute-start | bytes 1572872 | tf_op jit(solution)/shard_map/ppermute | solution.py:24
  101.2 22.9 %collective-permute-start.23 = (bf16[1792,512]{1,0:T(8,128)(2,1)S(1)}, bf16[1792,512]{1,0:T(8,128)(2,1)S(1)}, u32[]{:S(2)}, u32[]{:S(2)}) collective-permute-start(bf16[1792,512]{1,0:T(8,128)(2,1)S(1)} %copy-done), channel_id=1, source_target_pairs={{0,8},{8,0},{1,9},{9,1},{2,10},{10,2},{3,11},{11,3},{4,12},{12,4},... | collective-permute-start | bytes 5505032 | tf_op jit(solution)/shard_map/ppermute | solution.py:201
  101.5 16.5 %collective-permute-start.13 = (bf16[2,128,768]{2,1,0:T(8,128)(2,1)S(1)}, bf16[2,128,768]{2,1,0:T(8,128)(2,1)S(1)}, u32[]{:S(2)}, u32[]{:S(2)}) collective-permute-start(bf16[2,128,768]{2,1,0:T(8,128)(2,1)S(1)} %fusion.2), channel_id=1, source_target_pairs={{0,64},{16,80},{32,96},{48,112},{64,0},{80,16},{96,32},{112,48},{1... | collective-permute-start | bytes 1179656 | tf_op jit(solution)/shard_map/ppermute | solution.py:24
  118.4 10.7 %collective-permute-start.26 = (bf16[128,1792]{1,0:T(8,128)(2,1)S(1)}, bf16[128,1792]{1,0:T(8,128)(2,1)S(1)}, u32[]{:S(2)}, u32[]{:S(2)}) collective-permute-start(bf16[128,1792]{1,0:T(8,128)(2,1)S(1)} %pad_maximum_fusion.h0), channel_id=1, source_target_pairs={{0,48},{16,0},{32,16},{48,32},{64,112},{80,64},{96,80},{112,96},{1... | collective-permute-start | bytes 1376264 | tf_op jit(solution)/shard_map/ppermute | solution.py:24
  119.1 14.9 %collective-permute-start.28 = (bf16[128,1792]{1,0:T(8,128)(2,1)S(1)}, bf16[128,1792]{1,0:T(8,128)(2,1)S(1)}, u32[]{:S(2)}, u32[]{:S(2)}) collective-permute-start(bf16[128,1792]{1,0:T(8,128)(2,1)S(1)} %pad_maximum_fusion.h0), channel_id=1, source_target_pairs={{0,64},{16,80},{32,96},{48,112},{64,0},{80,16},{96,32},{112,48},{1... | collective-permute-start | bytes 1376264 | tf_op jit(solution)/shard_map/ppermute | solution.py:24
  121.6 23.1 %collective-permute-start.27 = (bf16[128,1792]{1,0:T(8,128)(2,1)S(1)}, bf16[128,1792]{1,0:T(8,128)(2,1)S(1)}, u32[]{:S(2)}, u32[]{:S(2)}) collective-permute-start(bf16[128,1792]{1,0:T(8,128)(2,1)S(1)} %pad_maximum_fusion.h0), channel_id=1, source_target_pairs={{0,112},{16,64},{32,80},{48,96},{64,48},{80,0},{96,16},{112,32},{1... | collective-permute-start | bytes 1376264 | tf_op jit(solution)/shard_map/ppermute | solution.py:24
  123.3 23.4 %collective-permute-start.24 = (bf16[128,1792]{1,0:T(8,128)(2,1)S(1)}, bf16[128,1792]{1,0:T(8,128)(2,1)S(1)}, u32[]{:S(2)}, u32[]{:S(2)}) collective-permute-start(bf16[128,1792]{1,0:T(8,128)(2,1)S(1)} %pad_maximum_fusion.h0), channel_id=1, source_target_pairs={{0,16},{16,32},{32,48},{48,0},{64,80},{80,96},{96,112},{112,64},{1... | collective-permute-start | bytes 1376264 | tf_op jit(solution)/shard_map/ppermute | solution.py:24
  124.1 31.7 %collective-permute-start.25 = (bf16[128,1792]{1,0:T(8,128)(2,1)S(1)}, bf16[128,1792]{1,0:T(8,128)(2,1)S(1)}, u32[]{:S(2)}, u32[]{:S(2)}) collective-permute-start(bf16[128,1792]{1,0:T(8,128)(2,1)S(1)} %pad_maximum_fusion.h0), channel_id=1, source_target_pairs={{0,80},{16,96},{32,112},{48,64},{64,16},{80,32},{96,48},{112,0},{1... | collective-permute-start | bytes 1376264 | tf_op jit(solution)/shard_map/ppermute | solution.py:24
  129.1 36.7 %collective-permute-start.21 = (bf16[128,1792]{1,0:T(8,128)(2,1)S(1)}, bf16[128,1792]{1,0:T(8,128)(2,1)S(1)}, u32[]{:S(2)}, u32[]{:S(2)}) collective-permute-start(bf16[128,1792]{1,0:T(8,128)(2,1)S(1)} %pad_maximum_fusion.h0), channel_id=1, source_target_pairs={{0,32},{16,48},{32,0},{48,16},{64,96},{80,112},{96,64},{112,80},{1... | collective-permute-start | bytes 1376264 | tf_op jit(solution)/shard_map/ppermute | solution.py:24
  134.0 31.8 %collective-permute-start.22 = (bf16[128,1792]{1,0:T(8,128)(2,1)S(1)}, bf16[128,1792]{1,0:T(8,128)(2,1)S(1)}, u32[]{:S(2)}, u32[]{:S(2)}) collective-permute-start(bf16[128,1792]{1,0:T(8,128)(2,1)S(1)} %pad_maximum_fusion.h0), channel_id=1, source_target_pairs={{0,96},{16,112},{32,64},{48,80},{64,32},{80,48},{96,0},{112,16},{1... | collective-permute-start | bytes 1376264 | tf_op jit(solution)/shard_map/ppermute | solution.py:24

commit v3 on v2

--- a/solution.py
+++ b/solution.py
@@ -11,8 +11,8 @@
 TP = ("y", "xl")
 SEQ = ("xh", "z", "c")
 SHAPE = {"xh": 2, "z": 4, "c": 2, "y": 4, "xl": 2}
-STEPS = (0, 1, 3, 2)
-PEERS = ((1, 0), (0, 3), (1, 3), (0, 1), (1, 1), (0, 2), (1, 2))
+STEPS = (1, 3, 2, 0)
+PEERS = ((0, 3), (1, 3), (0, 1), (1, 1), (0, 2), (1, 2), (1, 0))
 BF16, F32 = jnp.bfloat16, jnp.float32
 
 
@@ -96,33 +96,25 @@
         mine = pl.ds(pl.multiple_of(c * half, half), half)
         theirs = pl.ds(pl.multiple_of((1 - c) * half, half), half)
 
-        def product(n, own, other):
-            at = pl.ds(pl.multiple_of(n * tile, tile), tile)
-            x_mine = jnp.concatenate([near_ref[:, mine], far_ref[:, mine]], 0)
-            x_theirs = jnp.concatenate([near_ref[:, theirs], far_ref[:, theirs]], 0)
+        x_mine = jnp.concatenate([near_ref[:, mine], far_ref[:, mine]], 0)
+        x_theirs = jnp.concatenate([near_ref[:, theirs], far_ref[:, theirs]], 0)
+
+        def product(at, own, other):
             total = jnp.dot(x_mine, own[:, at], preferred_element_type=F32) + jnp.dot(
                 x_theirs, other[:, at], preferred_element_type=F32
             )
             return total.astype(BF16)
 
-        def to_one(n, _):
-            at = pl.ds(pl.multiple_of(n * tile, tile), tile)
-            for k, (a, b) in enumerate(((g0, g1), (u0, u1))):
-                total = product(n, a, b)
-                one[0, k, :, at] = total[:per]
-                one[1, k, :, at] = total[per:]
-            return 0
-
-        def to_two(n, _):
-            at = pl.ds(pl.multiple_of(n * tile, tile), tile)
-            for k, (a, b) in enumerate(((g0, g1), (u0, u1))):
-                total = product(n + first, a, b)
-                two_near[k, :, at] = total[:per]
-                two_far[k, :, at] = total[per:]
-            return 0
-
-        lax.fori_loop(0, first, to_one, 0)
-        lax.fori_loop(0, cols // tile - first, to_two, 0)
+        split = first * tile
+        for k, (a, b) in enumerate(((g0, g1), (u0, u1))):
+            for n in range(0, cols, tile):
+                total = product(slice(n, n + tile), a, b)
+                if n < split:
+                    one[0, k, :, n : n + tile] = total[:per]
+                    one[1, k, :, n : n + tile] = total[per:]
+                else:
+                    two_near[k, :, n - split : n - split + tile] = total[:per]
+                    two_far[k, :, n - split : n - split + tile] = total[per:]
 
     vmem = pl.BlockSpec(memory_space=pltpu.VMEM)
     two_shape = jax.ShapeDtypeStruct((2, per, cols - first * tile), BF16)
@@ -139,48 +131,55 @@
     )(place, near, far, own_gate, other_gate, own_up, other_up)
 
 
-def down(place, step, near, far, own, other, parts, terms):
-    per, depth = near.shape
-    half = own.shape[1]
+def down(place, step, left, right, own, other, parts, terms):
+    per = right[0].shape[0]
+    cut = left[0].shape[-1]
+    depth, half = own.shape
     sub = per // parts
-
-    def body(at_ref, h0, h1, d0, d1, *rest):
+    pair = len(left) == 1
+
+    def body(at_ref, *rest):
+        lefts, (r0, r1, d0, d1) = rest[: len(left)], rest[len(left) : len(left) + 4]
         out = rest[-1]
         c = at_ref[0]
         g = pl.program_id(0)
 
-        def write(h):
+        def write(l, r):
             for at, w in ((c, d0), (1 - c, d1)):
-                total = jnp.dot(h[...], w[...], preferred_element_type=F32).astype(BF16)
-                out[:, 0, :, pl.ds(pl.multiple_of(at * half, half), half)] = total.reshape(parts, sub, half)
+                total = jnp.dot(l, w[:cut], preferred_element_type=F32)
+                total = total + jnp.dot(r, w[cut:], preferred_element_type=F32)
+                out[:, 0, :, pl.ds(pl.multiple_of(at * half, half), half)] = total.astype(BF16).reshape(
+                    parts, sub, half
+                )
 
         @pl.when(g == 0)
         def _():
-            write(h0)
+            write(lefts[0][0] if pair else lefts[0][...], r0[...])
 
         @pl.when(g == 1)
         def _():
-            write(h1)
+            write(lefts[0][1] if pair else lefts[1][...], r1[...])
 
     def block(g, s):
         return (0, (s[1] + g) % 2 * 4 + (s[2] + step) % 4, 0, 0)
 
-    rows = weight = pl.BlockSpec(memory_space=pltpu.VMEM)
+    whole = pl.BlockSpec(memory_space=pltpu.VMEM)
     carried = [] if terms is None else [terms]
+    inputs = [*left, *right, own, other]
     return pl.pallas_call(
         body,
         grid_spec=pltpu.PrefetchScalarGridSpec(
             num_scalar_prefetch=1,
             grid=(2,),
-            in_specs=[rows, rows, weight, weight] + [pl.BlockSpec(memory_space=pl.ANY)] * len(carried),
+            in_specs=[whole] * len(inputs) + [pl.BlockSpec(memory_space=pl.ANY)] * len(carried),
             out_specs=pl.BlockSpec((parts, 1, sub, 2 * half), block),
         ),
         out_shape=jax.ShapeDtypeStruct((parts, 8, sub, 2 * half), BF16),
-        input_output_aliases={5: 0} if carried else {},
+        input_output_aliases={1 + len(inputs): 0} if carried else {},
         compiler_params=pltpu.CompilerParams(dimension_semantics=("arbitrary",), vmem_limit_bytes=12 * 2**20),
         cost_estimate=pl.CostEstimate(flops=8 * per * depth * half, bytes_accessed=4 * depth * half, transcendentals=0),
         name="down",
-    )(place, near, far, own, other, *carried)
+    )(place, *inputs, *carried)
 
 
 def total(*terms):
@@ -214,21 +213,29 @@
         if e:
             one_in[e] = hop(one[e], 0, e)
     two_in = {}
-    for e in STEPS[1:]:
+    for e in STEPS[:3]:
         both = total(near[e], far_in[e]).astype(BF16)
         two_in[e] = hop(both, 0, e)
-    firsts = [one[0]] + [one_in[e] for e in STEPS[1:]]
+    firsts = [one[0]] + [one_in[e] for e in STEPS[:3]]
     across = total(*[f[1] for f in firsts]).astype(BF16)
     last = hop(across, 1, 0)
-    left = total(*[f[0] for f in firsts], last)
-    right = total(near[0], far_in[0], *[two_in[e] for e in STEPS[1:]])
-    hidden = jnp.concatenate([swiglu(left), swiglu(right)], 1)
-    blocks = {(0, 0): hidden}
-    for dx, dz in PEERS:
-        blocks[dx, -dz % 4] = hop(hidden, dx, dz)
+    left = swiglu(total(*[f[0] for f in firsts], last))
+    left_far = hop(left, 1, 0)
+    right = swiglu(total(near[0], far_in[0], *[two_in[e] for e in STEPS[:3]]))
+    right_far = {0: hop(right, 1, 0)}
+    right_near = {0: right}
+    for e in STEPS[:3]:
+        right_near[e] = hop(right, 0, -e % 4)
+    pair = jnp.stack([left, left_far])
+    lefts = {0: (left, left_far)}
+    for e in STEPS[:3]:
+        lefts[e] = (hop(pair, 0, -e % 4),)
+    for e in STEPS[:3]:
+        right_far[e] = hop(right_near[e], 1, 0)
     terms = None
-    for e in STEPS:
-        terms = down(place, e, blocks[0, e], blocks[1, e], down_weight, down_other, parts, terms)
+    for e in (0, 1, 3, 2):
+        rights = (right_near[e], right_far[e])
+        terms = down(place, e, lefts[e], rights, down_weight, down_other, parts, terms)
     arrived = lax.all_to_all(terms, TP, split_axis=0, concat_axis=0, tiled=True)
     summed = arrived.astype(F32).sum(axis=0).astype(BF16)
     out = lax.all_to_all(summed, CHIPS, split_axis=0, concat_axis=0, tiled=True)

time: 212 us -> 201 us (0.948)
  waiting for transfers between devices: 74 us -> 67.8 us
  Pallas kernels: 31.4 us -> 27.3 us
    ppermute x25 -> x29, waiting for transfers between devices: 71 us -> 64.8 us  [hop(): return lax.ppermute(x, CHIPS, pairs)]
    pallas_call x4, Pallas kernels: 18.5 us -> 14.4 us  [gate_up(): pl.pallas_call(body, in_specs=[pl.BlockSpec(memory_space=pltpu.SMEM)] + [...]
    ppermute x25 -> x29, starting transfers between devices: 53.5 us -> 54.2 us  [hop(): return lax.ppermute(x, CHIPS, pairs)]
  transfers between devices with their start and end apart: 29 -> 33, of which waited for: 13 -> 12; matrix products, arithmetic and copies ran while one was open for 1% -> 1% of each run, Pallas kernels for 14% -> 13%
where the time goes in v3:
time: 201 us
  waiting for transfers between devices  67.8 us (34%)
  starting transfers between devices  56.7 us (28%)
  blocking collectives  41.4 us (21%)
  Pallas kernels  27.3 us (14%)
  local copies, waits for them, and re-layouts  4.9 us (2%)
  other arithmetic  2.34 us (1%)
    ppermute x29, waiting for transfers between devices, hop(): return lax.ppermute(x, CHIPS, pairs)  64.8 us
    ppermute x29, starting transfers between devices, hop(): return lax.ppermute(x, CHIPS, pairs)  54.2 us
    all_to_all x1, blocking collectives, shards(): arrived = lax.all_to_all(terms, TP, split_axis=0, concat_axis=0, tiled=True)  28.4 us
    pallas_call x4, Pallas kernels, gate_up(): pl.pallas_call(body, in_specs=[pl.BlockSpec(memory_space=pltpu.SMEM)] + [...  14.4 us
    all_to_all x1, blocking collectives, shards(): out = lax.all_to_all(summed, CHIPS, split_axis=0, concat_axis=0, tiled=True)  12.9 us
    pallas_call x4, Pallas kernels, down(): pl.pallas_call(body, grid_spec=pltpu.PrefetchScalarGridSpec(num_scalar_pr...  7.94 us
    pallas_call x1, Pallas kernels, conv_norm(): pl.pallas_call(body, grid_spec=pltpu.PrefetchScalarGridSpec(num_scalar_pr...  5.03 us
  transfers between devices with their start and end apart: 33, of which 12 were waited for; matrix products, arithmetic and copies ran while one was open for 1% of the time, Pallas kernels for 13%

profile of v3, /device:TPU:0, one launch (start us, length us, event | category | flops | bytes accessed | tf_op | source)
XLA Modules:
  0.0 200.7 jit_solution(6887006338376664656)
XLA Ops:
  0.5 0.9 slice.39
  1.4 1.9 collective-permute-start
  3.4 3.0 %collective-permute-done.edg = bf16[8,8192]{1,0:T(8,128)(2,1)S(1)} collective-permute-done((bf16[8,8192]{1,0:T(8,128)(2,1)S(1)}, bf16[8,8192]{1,0:T(8,128)(2,1)S(1)}, u32[]{:S(2)}, u32[]{:S(2)}) %collective-permute-start) | collective-permute-done | bytes 131104 | tf_op jit(solution)/shard_map/ppermute | solution.py:201
  6.4 1.6 copy-done.3
  8.0 0.9 copy-done.4
  9.7 5.0 %conv_norm.1 = (bf16[128,1024]{1,0:T(8,128)(2,1)S(1)}, bf16[128,1024]{1,0:T(8,128)(2,1)S(1)}, bf16[128,1024]{1,0:T(8,128)(2,1)S(1)}, bf16[128,1024]{1,0:T(8,128)...) custom-call(s32[3]{0:T(128)S(1)} %pad_add_fusion.at_ref, ...), custom_call_target="tpu_custom_call" | custom-call | flops 4000000000 | bytes 4194304 | tf_op jit(solution)/shard_map/conv_norm/pallas_call | solution.py:67
  14.7 5.5 %collective-permute-start.4 = (bf16[128,1024]{1,0:T(8,128)(2,1)S(1)}, bf16[128,1024]{1,0:T(8,128)(2,1)S(1)}, u32[]{:S(2)}, u32[]{:S(2)}) collective-permute-start(bf16[128,1024]{1,0:T(8,128)(2,1)S(1)} %get-tuple-element.28), channel_id=1, source_target_pairs={{0,48},{16,0},{32,16},{48,32},{64,112},{80,64},{96,80},{112,96},{1... | collective-permute-start | bytes 786440 | tf_op jit(solution)/shard_map/ppermute | solution.py:24
  20.2 2.9 %collective-permute-start.5 = (bf16[128,1024]{1,0:T(8,128)(2,1)S(1)}, bf16[128,1024]{1,0:T(8,128)(2,1)S(1)}, u32[]{:S(2)}, u32[]{:S(2)}) collective-permute-start(bf16[128,1024]{1,0:T(8,128)(2,1)S(1)} %get-tuple-element.29), channel_id=1, source_target_pairs={{0,112},{16,64},{32,80},{48,96},{64,48},{80,0},{96,16},{112,32},{1... | collective-permute-start | bytes 786440 | tf_op jit(solution)/shard_map/ppermute | solution.py:24
  23.1 1.6 collective-permute-start.7
  24.7 6.2 %collective-permute-done.4.near_ref = bf16[128,1024]{1,0:T(8,128)(2,1)S(1)} collective-permute-done((bf16[128,1024]{1,0:T(8,128)(2,1)S(1)}, bf16[128,1024]{1,0:T(8,128)(2,1)S(1)}, u32[]{:S(2)}, u32[]{:S(2)}) %collective-permute-start.4) | collective-permute-done | bytes 262176 | tf_op jit(solution)/shard_map/ppermute | solution.py:24
  30.9 3.1 %collective-permute-start.8 = (bf16[128,1024]{1,0:T(8,128)(2,1)S(1)}, bf16[128,1024]{1,0:T(8,128)(2,1)S(1)}, u32[]{:S(2)}, u32[]{:S(2)}) collective-permute-start(bf16[128,1024]{1,0:T(8,128)(2,1)S(1)} %get-tuple-element.32), channel_id=1, source_target_pairs={{0,80},{16,96},{32,112},{48,64},{64,16},{80,32},{96,48},{112,0},{1... | collective-permute-start | bytes 786440 | tf_op jit(solution)/shard_map/ppermute | solution.py:24
  34.0 4.3 %collective-permute-start.10 = (bf16[128,1024]{1,0:T(8,128)(2,1)S(1)}, bf16[128,1024]{1,0:T(8,128)(2,1)S(1)}, u32[]{:S(2)}, u32[]{:S(2)}) collective-permute-start(bf16[128,1024]{1,0:T(8,128)(2,1)S(1)} %get-tuple-element.34), channel_id=1, source_target_pairs={{0,32},{16,48},{32,0},{48,16},{64,96},{80,112},{96,64},{112,80},{1... | collective-permute-start | bytes 786440 | tf_op jit(solution)/shard_map/ppermute | solution.py:24
  38.6 2.8 %collective-permute-start.1 = (bf16[128,1024]{1,0:T(8,128)(2,1)S(1)}, bf16[128,1024]{1,0:T(8,128)(2,1)S(1)}, u32[]{:S(2)}, u32[]{:S(2)}) collective-permute-start(bf16[128,1024]{1,0:T(8,128)(2,1)S(1)} %get-tuple-element.26), channel_id=1, source_target_pairs={{0,64},{16,80},{32,96},{48,112},{64,0},{80,16},{96,32},{112,48},{1... | collective-permute-start | bytes 786440 | tf_op jit(solution)/shard_map/ppermute | solution.py:24
  41.4 3.6 %gate_up.5 = (bf16[2,2,128,768]{3,2,1,0:T(8,128)(2,1)S(1)}, bf16[2,128,1024]{2,1,0:T(8,128)(2,1)S(1)}, bf16[2,128,1024]{2,1,0:T(8,128)(2,1)S(1)}) custom-call(s32[3]{0:T(128)S(1)} %pad_add_fusion.at_ref, bf16[128,1024]{1,0:T(8,128)(2,1)S(1)} %collective-permute-done.4.near_ref, bf16[128,1024]{1,0:T(8,128)(2,1)S(1)} %collective-permute-done.5.far_ref, ...), custom_call_target="tpu_custom_call" | custom-call | flops 1879048192 | bytes 7340032 | tf_op jit(solution)/shard_map/gate_up/pallas_call | solution.py:121
  45.0 0.8 collective-permute-start.17
  45.8 3.6 %gate_up.6 = (bf16[2,2,128,768]{3,2,1,0:T(8,128)(2,1)S(1)}, bf16[2,128,1024]{2,1,0:T(8,128)(2,1)S(1)}, bf16[2,128,1024]{2,1,0:T(8,128)(2,1)S(1)}) custom-call(s32[3]{0:T(128)S(1)} %pad_add_fusion.at_ref, bf16[128,1024]{1,0:T(8,128)(2,1)S(1)} %collective-permute-done.7.near_ref, bf16[128,1024]{1,0:T(8,128)(2,1)S(1)} %collective-permute-done.8.far_ref, ...), custom_call_target="tpu_custom_call" | custom-call | flops 1879048192 | bytes 7340032 | tf_op jit(solution)/shard_map/gate_up/pallas_call | solution.py:121
  49.4 2.9 %collective-permute-start.19 = (bf16[2,128,1024]{2,1,0:T(8,128)(2,1)S(1)}, bf16[2,128,1024]{2,1,0:T(8,128)(2,1)S(1)}, u32[]{:S(2)}, u32[]{:S(2)}) collective-permute-start(bf16[2,128,1024]{2,1,0:T(8,128)(2,1)S(1)} %get-tuple-element.42), channel_id=1, source_target_pairs={{0,64},{16,80},{32,96},{48,112},{64,0},{80,16},{96,32},{112,48},{1... | collective-permute-start | bytes 1572872 | tf_op jit(solution)/shard_map/ppermute | solution.py:24
  52.3 1.7 collective-permute-done.10.near_ref
  54.0 3.6 %gate_up.7 = (bf16[2,2,128,768]{3,2,1,0:T(8,128)(2,1)S(1)}, bf16[2,128,1024]{2,1,0:T(8,128)(2,1)S(1)}, bf16[2,128,1024]{2,1,0:T(8,128)(2,1)S(1)}) custom-call(s32[3]{0:T(128)S(1)} %pad_add_fusion.at_ref, bf16[128,1024]{1,0:T(8,128)(2,1)S(1)} %collective-permute-done.10.near_ref, bf16[128,1024]{1,0:T(8,128)(2,1)S(1)} %collective-permute-done.11.far_ref, ...), custom_call_target="tpu_custom_call" | custom-call | flops 1879048192 | bytes 7340032 | tf_op jit(solution)/shard_map/gate_up/pallas_call | solution.py:121
  57.6 1.6 collective-permute-start.21
  59.1 3.2 %collective-permute-start.9 = (bf16[2,2,128,768]{3,2,1,0:T(8,128)(2,1)S(1)}, bf16[2,2,128,768]{3,2,1,0:T(8,128)(2,1)S(1)}, u32[]{:S(2)}, u32[]{:S(2)}) collective-permute-start(bf16[2,2,128,768]{3,2,1,0:T(8,128)(2,1)S(1)} %get-tuple-element.33), channel_id=1, source_target_pairs={{0,48},{16,0},{32,16},{48,32},{64,112},{80,64},{96,80},{112,96},{1... | collective-permute-start | bytes 2359304 | tf_op jit(solution)/shard_map/ppermute | solution.py:24
  62.4 3.6 %gate_up.4 = (bf16[2,2,128,768]{3,2,1,0:T(8,128)(2,1)S(1)}, bf16[2,128,1024]{2,1,0:T(8,128)(2,1)S(1)}, bf16[2,128,1024]{2,1,0:T(8,128)(2,1)S(1)}) custom-call(s32[3]{0:T(128)S(1)} %pad_add_fusion.at_ref, bf16[128,1024]{1,0:T(8,128)(2,1)S(1)} %get-tuple-element.25.near_ref, bf16[128,1024]{1,0:T(8,128)(2,1)S(1)} %collective-permute-done.1.far_ref, ...), custom_call_target="tpu_custom_call" | custom-call | flops 1879048192 | bytes 7340032 | tf_op jit(solution)/shard_map/gate_up/pallas_call | solution.py:121
  66.0 2.8 %collective-permute-start.12 = (bf16[2,2,128,768]{3,2,1,0:T(8,128)(2,1)S(1)}, bf16[2,2,128,768]{3,2,1,0:T(8,128)(2,1)S(1)}, u32[]{:S(2)}, u32[]{:S(2)}) collective-permute-start(bf16[2,2,128,768]{3,2,1,0:T(8,128)(2,1)S(1)} %get-tuple-element.36), channel_id=1, source_target_pairs={{0,32},{16,48},{32,0},{48,16},{64,96},{80,112},{96,64},{112,80},{1... | collective-permute-start | bytes 2359304 | tf_op jit(solution)/shard_map/ppermute | solution.py:24
  69.0 7.5 %collective-permute-done.19 = bf16[2,128,1024]{2,1,0:T(8,128)(2,1)S(1)} collective-permute-done((bf16[2,128,1024]{2,1,0:T(8,128)(2,1)S(1)}, bf16[2,128,1024]{2,1,0:T(8,128)(2,1)S(1)}, u32[]{:S(2)}, u32[]{:S(2)}) %collective-permute-start.19) | collective-permute-done | bytes 524320 | tf_op jit(solution)/shard_map/ppermute | solution.py:24
  76.6 1.2 collective-permute-start.16
  78.0 9.8 %collective-permute-done.21 = bf16[2,128,1024]{2,1,0:T(8,128)(2,1)S(1)} collective-permute-done((bf16[2,128,1024]{2,1,0:T(8,128)(2,1)S(1)}, bf16[2,128,1024]{2,1,0:T(8,128)(2,1)S(1)}, u32[]{:S(2)}, u32[]{:S(2)}) %collective-permute-start.21) | collective-permute-done | bytes 524320 | tf_op jit(solution)/shard_map/ppermute | solution.py:24
  87.8 0.8 collective-permute-start.18
  88.8 7.0 %collective-permute-done.6 = bf16[2,2,128,768]{3,2,1,0:T(8,128)(2,1)S(1)} collective-permute-done((bf16[2,2,128,768]{3,2,1,0:T(8,128)(2,1)S(1)}, bf16[2,2,128,768]{3,2,1,0:T(8,128)(2,1)S(1)}, u32[]{:S(2)}, u32[]{:S(2)}) %collective-permute-start.6) | collective-permute-done | bytes 786464 | tf_op jit(solution)/shard_map/ppermute | solution.py:24
  96.2 3.9 %collective-permute-start.13 = (bf16[2,128,768]{2,1,0:T(8,128)(2,1)S(1)}, bf16[2,128,768]{2,1,0:T(8,128)(2,1)S(1)}, u32[]{:S(2)}, u32[]{:S(2)}) collective-permute-start(bf16[2,128,768]{2,1,0:T(8,128)(2,1)S(1)} %fusion.2), channel_id=1, source_target_pairs={{0,64},{16,80},{32,96},{48,112},{64,0},{80,16},{96,32},{112,48},{1... | collective-permute-start | bytes 1179656 | tf_op jit(solution)/shard_map/ppermute | solution.py:24
  100.1 17.2 %collective-permute-done.18 = bf16[2,128,1024]{2,1,0:T(8,128)(2,1)S(1)} collective-permute-done((bf16[2,128,1024]{2,1,0:T(8,128)(2,1)S(1)}, bf16[2,128,1024]{2,1,0:T(8,128)(2,1)S(1)}, u32[]{:S(2)}, u32[]{:S(2)}) %collective-permute-start.18) | collective-permute-done | bytes 524320 | tf_op jit(solution)/shard_map/ppermute | solution.py:24
  117.9 3.2 %collective-permute-start.32 = (bf16[128,1024]{1,0:T(8,128)(2,1)S(1)}, bf16[128,1024]{1,0:T(8,128)(2,1)S(1)}, u32[]{:S(2)}, u32[]{:S(2)}) collective-permute-start(bf16[128,1024]{1,0:T(8,128)(2,1)S(1)} %fusion.1.rest_2_), channel_id=1, source_target_pairs={{0,64},{16,80},{32,96},{48,112},{64,0},{80,16},{96,32},{112,48},{1... | collective-permute-start | bytes 786440 | tf_op jit(solution)/shard_map/ppermute | solution.py:24
  121.2 3.0 %collective-permute-start.30 = (bf16[128,1024]{1,0:T(8,128)(2,1)S(1)}, bf16[128,1024]{1,0:T(8,128)(2,1)S(1)}, u32[]{:S(2)}, u32[]{:S(2)}) collective-permute-start(bf16[128,1024]{1,0:T(8,128)(2,1)S(1)} %fusion.1.rest_2_), channel_id=1, source_target_pairs={{0,48},{16,0},{32,16},{48,32},{64,112},{80,64},{96,80},{112,96},{1... | collective-permute-start | bytes 786440 | tf_op jit(solution)/shard_map/ppermute | solution.py:24
  125.1 6.7 %collective-permute-done.14.rest_1_ = bf16[128,768]{1,0:T(8,128)(2,1)S(1)} collective-permute-done((bf16[128,768]{1,0:T(8,128)(2,1)S(1)}, bf16[128,768]{1,0:T(8,128)(2,1)S(1)}, u32[]{:S(2)}, u32[]{:S(2)}) %collective-permute-start.14) | collective-permute-done | bytes 196640 | tf_op jit(solution)/shard_map/ppermute | solution.py:24
  131.8 1.5 collective-permute-start.23
  133.3 1.8 collective-permute-start.29
  135.1 1.2 collective-permute-start.31
  136.6 2.6 %collective-permute-start.15 = (bf16[2,128,768]{2,1,0:T(8,128)(2,1)S(1)}, bf16[2,128,768]{2,1,0:T(8,128)(2,1)S(1)}, u32[]{:S(2)}, u32[]{:S(2)}) collective-permute-start(bf16[2,128,768]{2,1,0:T(8,128)(2,1)S(1)} %pad_maximum_fusion), channel_id=1, source_target_pairs={{0,32},{16,48},{32,0},{48,16},{64,96},{80,112},{96,64},{112,80},{1... | collective-permute-start | bytes 1179656 | tf_op jit(solution)/shard_map/ppermute | solution.py:24
  139.3 3.2 %collective-permute-done.23.rest_1_ = bf16[128,1024]{1,0:T(8,128)(2,1)S(1)} collective-permute-done((bf16[128,1024]{1,0:T(8,128)(2,1)S(1)}, bf16[128,1024]{1,0:T(8,128)(2,1)S(1)}, u32[]{:S(2)}, u32[]{:S(2)}) %collective-permute-start.23) | collective-permute-done | bytes 262176 | tf_op jit(solution)/shard_map/ppermute | solution.py:24
  142.4 1.8 collective-permute-start.28
  144.2 1.6 collective-permute-done.31.rest_2_
  146.5 2.0 down.4.rest_5_
  148.5 2.2 %collective-permute-done.29.rest_0_ = bf16[2,128,768]{2,1,0:T(8,128)(2,1)S(1)} collective-permute-done((bf16[2,128,768]{2,1,0:T(8,128)(2,1)S(1)}, bf16[2,128,768]{2,1,0:T(8,128)(2,1)S(1)}, u32[]{:S(2)}, u32[]{:S(2)}) %collective-permute-start.29) | collective-permute-done | bytes 393248 | tf_op jit(solution)/shard_map/ppermute | solution.py:24
  150.7 2.0 down.5.rest_5_
  152.7 2.0 down.6.rest_5_
  154.7 1.6 collective-permute-done.15.rest_0_
  156.3 2.0 down.7
  158.3 28.4 %all_to_all.10 = bf16[8,8,16,1024]{3,2,1,0:T(8,128)(2,1)S(1)} all-to-all(bf16[8,8,16,1024]{3,2,1,0:T(8,128)(2,1)S(1)} %down.7), channel_id=1, replica_groups=mesh['xh'=2,'z'=4,'c'=2,'y'=4,'xl'=2] {'y','xl'}, dimensions={0} | all-to-all | bytes 4194304 | tf_op jit(solution)/shard_map/all_to_all | solution.py:239
  187.0 12.9 %all_to_all.11 = bf16[8,16,1024]{2,1,0:T(8,128)(2,1)S(1)} all-to-all(bf16[8,16,1024]{2,1,0:T(8,128)(2,1)S(1)} %reduce_sum.12), channel_id=1, replica_groups=mesh['xh'=2,'z'=4,'c'=2,'y'=4,'xl'=2] {'xh','z'}, dimensions={0} | all-to-all | bytes 524288 | tf_op jit(solution)/shard_map/all_to_all | solution.py:241
  (55 shorter events, 6.1 us)
Async XLA Ops:
  0.0 38.3 %collective-permute-start.2 = (bf16[512,1792]{1,0:T(8,128)(2,1)}, bf16[512,1792]{1,0:T(8,128)(2,1)S(1)}, u32[]{:S(2)}, u32[]{:S(2)}) collective-permute-start(bf16[512,1792]{1,0:T(8,128)(2,1)} %g0.7), channel_id=1, source_target_pairs={{0,8},{8,0},{1,9},{9,1},{2,10},{10,2},{3,11},{11,3},{4,12},{12,4},... | collective-permute-start | bytes 5505032 | tf_op jit(solution)/shard_map/ppermute | solution.py:200
  0.0 38.6 %collective-permute-start.3 = (bf16[512,1792]{1,0:T(8,128)(2,1)}, bf16[512,1792]{1,0:T(8,128)(2,1)}, u32[]{:S(2)}, u32[]{:S(2)}) collective-permute-start(bf16[512,1792]{1,0:T(8,128)(2,1)} %u0.7), channel_id=1, source_target_pairs={{0,8},{8,0},{1,9},{9,1},{2,10},{10,2},{3,11},{11,3},{4,12},{12,4},... | collective-permute-start | bytes 5505032 | tf_op jit(solution)/shard_map/ppermute | solution.py:200
  1.4 5.0 %collective-permute-start = (bf16[8,8192]{1,0:T(8,128)(2,1)S(1)}, bf16[8,8192]{1,0:T(8,128)(2,1)S(1)}, u32[]{:S(2)}, u32[]{:S(2)}) collective-permute-start(bf16[8,8192]{1,0:T(8,128)(2,1)S(1)} %slice.39), channel_id=1, source_target_pairs={{0,8},{8,16},{16,24},{24,32},{32,40},{40,48},{48,56},{56,64},{64,7... | collective-permute-start | bytes 393224 | tf_op jit(solution)/shard_map/ppermute | solution.py:201
  6.4 1.6 copy-start.3
  8.0 0.9 copy-start.4
  8.9 0.8 copy-start.5
  9.7 31.7 %copy-start.1 = (bf16[512,1792]{1,0:T(8,128)(2,1)S(1)}, bf16[512,1792]{1,0:T(8,128)(2,1)}, u32[]{:S(2)}) copy-start(bf16[512,1792]{1,0:T(8,128)(2,1)} %g0.7) | copy-start | bytes 5505028
  9.7 31.7 %copy-start.2 = (bf16[512,1792]{1,0:T(8,128)(2,1)S(1)}, bf16[512,1792]{1,0:T(8,128)(2,1)}, u32[]{:S(2)}) copy-start(bf16[512,1792]{1,0:T(8,128)(2,1)} %u0.7) | copy-start | bytes 5505028
  14.7 16.2 %collective-permute-start.4 = (bf16[128,1024]{1,0:T(8,128)(2,1)S(1)}, bf16[128,1024]{1,0:T(8,128)(2,1)S(1)}, u32[]{:S(2)}, u32[]{:S(2)}) collective-permute-start(bf16[128,1024]{1,0:T(8,128)(2,1)S(1)} %get-tuple-element.28), channel_id=1, source_target_pairs={{0,48},{16,0},{32,16},{48,32},{64,112},{80,64},{96,80},{112,96},{1... | collective-permute-start | bytes 786440 | tf_op jit(solution)/shard_map/ppermute | solution.py:24
  20.2 13.8 %collective-permute-start.5 = (bf16[128,1024]{1,0:T(8,128)(2,1)S(1)}, bf16[128,1024]{1,0:T(8,128)(2,1)S(1)}, u32[]{:S(2)}, u32[]{:S(2)}) collective-permute-start(bf16[128,1024]{1,0:T(8,128)(2,1)S(1)} %get-tuple-element.29), channel_id=1, source_target_pairs={{0,112},{16,64},{32,80},{48,96},{64,48},{80,0},{96,16},{112,32},{1... | collective-permute-start | bytes 786440 | tf_op jit(solution)/shard_map/ppermute | solution.py:24
  23.1 21.9 %collective-permute-start.7 = (bf16[128,1024]{1,0:T(8,128)(2,1)S(1)}, bf16[128,1024]{1,0:T(8,128)(2,1)S(1)}, u32[]{:S(2)}, u32[]{:S(2)}) collective-permute-start(bf16[128,1024]{1,0:T(8,128)(2,1)S(1)} %get-tuple-element.31), channel_id=1, source_target_pairs={{0,16},{16,32},{32,48},{48,0},{64,80},{80,96},{96,112},{112,64},{1... | collective-permute-start | bytes 786440 | tf_op jit(solution)/shard_map/ppermute | solution.py:24
  30.9 14.9 %collective-permute-start.8 = (bf16[128,1024]{1,0:T(8,128)(2,1)S(1)}, bf16[128,1024]{1,0:T(8,128)(2,1)S(1)}, u32[]{:S(2)}, u32[]{:S(2)}) collective-permute-start(bf16[128,1024]{1,0:T(8,128)(2,1)S(1)} %get-tuple-element.32), channel_id=1, source_target_pairs={{0,80},{16,96},{32,112},{48,64},{64,16},{80,32},{96,48},{112,0},{1... | collective-permute-start | bytes 786440 | tf_op jit(solution)/shard_map/ppermute | solution.py:24
  34.0 20.0 %collective-permute-start.10 = (bf16[128,1024]{1,0:T(8,128)(2,1)S(1)}, bf16[128,1024]{1,0:T(8,128)(2,1)S(1)}, u32[]{:S(2)}, u32[]{:S(2)}) collective-permute-start(bf16[128,1024]{1,0:T(8,128)(2,1)S(1)} %get-tuple-element.34), channel_id=1, source_target_pairs={{0,32},{16,48},{32,0},{48,16},{64,96},{80,112},{96,64},{112,80},{1... | collective-permute-start | bytes 786440 | tf_op jit(solution)/shard_map/ppermute | solution.py:24
  38.3 15.7 %collective-permute-start.11 = (bf16[128,1024]{1,0:T(8,128)(2,1)S(1)}, bf16[128,1024]{1,0:T(8,128)(2,1)S(1)}, u32[]{:S(2)}, u32[]{:S(2)}) collective-permute-start(bf16[128,1024]{1,0:T(8,128)(2,1)S(1)} %get-tuple-element.35), channel_id=1, source_target_pairs={{0,96},{16,112},{32,64},{48,80},{64,32},{80,48},{96,0},{112,16},{1... | collective-permute-start | bytes 786440 | tf_op jit(solution)/shard_map/ppermute | solution.py:24
  38.6 20.6 %collective-permute-start.1 = (bf16[128,1024]{1,0:T(8,128)(2,1)S(1)}, bf16[128,1024]{1,0:T(8,128)(2,1)S(1)}, u32[]{:S(2)}, u32[]{:S(2)}) collective-permute-start(bf16[128,1024]{1,0:T(8,128)(2,1)S(1)} %get-tuple-element.26), channel_id=1, source_target_pairs={{0,64},{16,80},{32,96},{48,112},{64,0},{80,16},{96,32},{112,48},{1... | collective-permute-start | bytes 786440 | tf_op jit(solution)/shard_map/ppermute | solution.py:24
  45.0 21.0 %collective-permute-start.17 = (bf16[2,128,1024]{2,1,0:T(8,128)(2,1)S(1)}, bf16[2,128,1024]{2,1,0:T(8,128)(2,1)S(1)}, u32[]{:S(2)}, u32[]{:S(2)}) collective-permute-start(bf16[2,128,1024]{2,1,0:T(8,128)(2,1)S(1)} %get-tuple-element.40), channel_id=1, source_target_pairs={{0,64},{16,80},{32,96},{48,112},{64,0},{80,16},{96,32},{112,48},{1... | collective-permute-start | bytes 1572872 | tf_op jit(solution)/shard_map/ppermute | solution.py:24
  49.4 27.2 %collective-permute-start.19 = (bf16[2,128,1024]{2,1,0:T(8,128)(2,1)S(1)}, bf16[2,128,1024]{2,1,0:T(8,128)(2,1)S(1)}, u32[]{:S(2)}, u32[]{:S(2)}) collective-permute-start(bf16[2,128,1024]{2,1,0:T(8,128)(2,1)S(1)} %get-tuple-element.42), channel_id=1, source_target_pairs={{0,64},{16,80},{32,96},{48,112},{64,0},{80,16},{96,32},{112,48},{1... | collective-permute-start | bytes 1572872 | tf_op jit(solution)/shard_map/ppermute | solution.py:24
  57.6 30.3 %collective-permute-start.21 = (bf16[2,128,1024]{2,1,0:T(8,128)(2,1)S(1)}, bf16[2,128,1024]{2,1,0:T(8,128)(2,1)S(1)}, u32[]{:S(2)}, u32[]{:S(2)}) collective-permute-start(bf16[2,128,1024]{2,1,0:T(8,128)(2,1)S(1)} %get-tuple-element.44), channel_id=1, source_target_pairs={{0,64},{16,80},{32,96},{48,112},{64,0},{80,16},{96,32},{112,48},{1... | collective-permute-start | bytes 1572872 | tf_op jit(solution)/shard_map/ppermute | solution.py:24
  59.1 36.7 %collective-permute-start.6 = (bf16[2,2,128,768]{3,2,1,0:T(8,128)(2,1)S(1)}, bf16[2,2,128,768]{3,2,1,0:T(8,128)(2,1)S(1)}, u32[]{:S(2)}, u32[]{:S(2)}) collective-permute-start(bf16[2,2,128,768]{3,2,1,0:T(8,128)(2,1)S(1)} %get-tuple-element.30), channel_id=1, source_target_pairs={{0,16},{16,32},{32,48},{48,0},{64,80},{80,96},{96,112},{112,64},{1... | collective-permute-start | bytes 2359304 | tf_op jit(solution)/shard_map/ppermute | solution.py:24
  59.1 36.7 %collective-permute-start.9 = (bf16[2,2,128,768]{3,2,1,0:T(8,128)(2,1)S(1)}, bf16[2,2,128,768]{3,2,1,0:T(8,128)(2,1)S(1)}, u32[]{:S(2)}, u32[]{:S(2)}) collective-permute-start(bf16[2,2,128,768]{3,2,1,0:T(8,128)(2,1)S(1)} %get-tuple-element.33), channel_id=1, source_target_pairs={{0,48},{16,0},{32,16},{48,32},{64,112},{80,64},{96,80},{112,96},{1... | collective-permute-start | bytes 2359304 | tf_op jit(solution)/shard_map/ppermute | solution.py:24
  66.0 29.9 %collective-permute-start.12 = (bf16[2,2,128,768]{3,2,1,0:T(8,128)(2,1)S(1)}, bf16[2,2,128,768]{3,2,1,0:T(8,128)(2,1)S(1)}, u32[]{:S(2)}, u32[]{:S(2)}) collective-permute-start(bf16[2,2,128,768]{3,2,1,0:T(8,128)(2,1)S(1)} %get-tuple-element.36), channel_id=1, source_target_pairs={{0,32},{16,48},{32,0},{48,16},{64,96},{80,112},{96,64},{112,80},{1... | collective-permute-start | bytes 2359304 | tf_op jit(solution)/shard_map/ppermute | solution.py:24
  68.8 27.1 %copy-start = (bf16[1792,512]{1,0:T(8,128)(2,1)S(1)}, bf16[1792,512]{1,0:T(8,128)(2,1)}, u32[]{:S(2)}) copy-start(bf16[1792,512]{1,0:T(8,128)(2,1)} %rest_3_.5) | copy-start | bytes 5505028
  76.6 19.6 %collective-permute-start.16 = (bf16[2,128,1024]{2,1,0:T(8,128)(2,1)S(1)}, bf16[2,128,1024]{2,1,0:T(8,128)(2,1)S(1)}, u32[]{:S(2)}, u32[]{:S(2)}) collective-permute-start(bf16[2,128,1024]{2,1,0:T(8,128)(2,1)S(1)} %get-tuple-element.38), channel_id=1, source_target_pairs={{0,64},{16,80},{32,96},{48,112},{64,0},{80,16},{96,32},{112,48},{1... | collective-permute-start | bytes 1572872 | tf_op jit(solution)/shard_map/ppermute | solution.py:24
  87.8 29.5 %collective-permute-start.18 = (bf16[2,128,1024]{2,1,0:T(8,128)(2,1)S(1)}, bf16[2,128,1024]{2,1,0:T(8,128)(2,1)S(1)}, u32[]{:S(2)}, u32[]{:S(2)}) collective-permute-start(bf16[2,128,1024]{2,1,0:T(8,128)(2,1)S(1)} %add_convert_fusion.2), channel_id=1, source_target_pairs={{0,16},{16,32},{32,48},{48,0},{64,80},{80,96},{96,112},{112,64},{1... | collective-permute-start | bytes 1572872 | tf_op jit(solution)/shard_map/ppermute | solution.py:24
  95.9 21.4 %collective-permute-start.20 = (bf16[2,128,1024]{2,1,0:T(8,128)(2,1)S(1)}, bf16[2,128,1024]{2,1,0:T(8,128)(2,1)S(1)}, u32[]{:S(2)}, u32[]{:S(2)}) collective-permute-start(bf16[2,128,1024]{2,1,0:T(8,128)(2,1)S(1)} %add_convert_fusion.1), channel_id=1, source_target_pairs={{0,48},{16,0},{32,16},{48,32},{64,112},{80,64},{96,80},{112,96},{1... | collective-permute-start | bytes 1572872 | tf_op jit(solution)/shard_map/ppermute | solution.py:24
  95.9 21.4 %collective-permute-start.22 = (bf16[2,128,1024]{2,1,0:T(8,128)(2,1)S(1)}, bf16[2,128,1024]{2,1,0:T(8,128)(2,1)S(1)}, u32[]{:S(2)}, u32[]{:S(2)}) collective-permute-start(bf16[2,128,1024]{2,1,0:T(8,128)(2,1)S(1)} %add_convert_fusion), channel_id=1, source_target_pairs={{0,32},{16,48},{32,0},{48,16},{64,96},{80,112},{96,64},{112,80},{1... | collective-permute-start | bytes 1572872 | tf_op jit(solution)/shard_map/ppermute | solution.py:24
  95.9 37.4 %collective-permute-start.25 = (bf16[1792,512]{1,0:T(8,128)(2,1)S(1)}, bf16[1792,512]{1,0:T(8,128)(2,1)S(1)}, u32[]{:S(2)}, u32[]{:S(2)}) collective-permute-start(bf16[1792,512]{1,0:T(8,128)(2,1)S(1)} %copy-done), channel_id=1, source_target_pairs={{0,8},{8,0},{1,9},{9,1},{2,10},{10,2},{3,11},{11,3},{4,12},{12,4},... | collective-permute-start | bytes 5505032 | tf_op jit(solution)/shard_map/ppermute | solution.py:200
  96.2 27.9 %collective-permute-start.13 = (bf16[2,128,768]{2,1,0:T(8,128)(2,1)S(1)}, bf16[2,128,768]{2,1,0:T(8,128)(2,1)S(1)}, u32[]{:S(2)}, u32[]{:S(2)}) collective-permute-start(bf16[2,128,768]{2,1,0:T(8,128)(2,1)S(1)} %fusion.2), channel_id=1, source_target_pairs={{0,64},{16,80},{32,96},{48,112},{64,0},{80,16},{96,32},{112,48},{1... | collective-permute-start | bytes 1179656 | tf_op jit(solution)/shard_map/ppermute | solution.py:24
  117.9 18.5 %collective-permute-start.32 = (bf16[128,1024]{1,0:T(8,128)(2,1)S(1)}, bf16[128,1024]{1,0:T(8,128)(2,1)S(1)}, u32[]{:S(2)}, u32[]{:S(2)}) collective-permute-start(bf16[128,1024]{1,0:T(8,128)(2,1)S(1)} %fusion.1.rest_2_), channel_id=1, source_target_pairs={{0,64},{16,80},{32,96},{48,112},{64,0},{80,16},{96,32},{112,48},{1... | collective-permute-start | bytes 786440 | tf_op jit(solution)/shard_map/ppermute | solution.py:24
  121.2 14.0 %collective-permute-start.30 = (bf16[128,1024]{1,0:T(8,128)(2,1)S(1)}, bf16[128,1024]{1,0:T(8,128)(2,1)S(1)}, u32[]{:S(2)}, u32[]{:S(2)}) collective-permute-start(bf16[128,1024]{1,0:T(8,128)(2,1)S(1)} %fusion.1.rest_2_), channel_id=1, source_target_pairs={{0,48},{16,0},{32,16},{48,32},{64,112},{80,64},{96,80},{112,96},{1... | collective-permute-start | bytes 786440 | tf_op jit(solution)/shard_map/ppermute | solution.py:24
  124.1 12.5 %collective-permute-start.27 = (bf16[128,1024]{1,0:T(8,128)(2,1)S(1)}, bf16[128,1024]{1,0:T(8,128)(2,1)S(1)}, u32[]{:S(2)}, u32[]{:S(2)}) collective-permute-start(bf16[128,1024]{1,0:T(8,128)(2,1)S(1)} %fusion.1.rest_2_), channel_id=1, source_target_pairs={{0,16},{16,32},{32,48},{48,0},{64,80},{80,96},{96,112},{112,64},{1... | collective-permute-start | bytes 786440 | tf_op jit(solution)/shard_map/ppermute | solution.py:24
  124.5 7.3 %collective-permute-start.14 = (bf16[128,768]{1,0:T(8,128)(2,1)S(1)}, bf16[128,768]{1,0:T(8,128)(2,1)S(1)}, u32[]{:S(2)}, u32[]{:S(2)}) collective-permute-start(bf16[128,768]{1,0:T(8,128)(2,1)S(1)} %fusion.3.rest_0_), channel_id=1, source_target_pairs={{0,64},{16,80},{32,96},{48,112},{64,0},{80,16},{96,32},{112,48},{1... | collective-permute-start | bytes 589832 | tf_op jit(solution)/shard_map/ppermute | solution.py:24
  131.8 10.7 %collective-permute-start.23 = (bf16[128,1024]{1,0:T(8,128)(2,1)S(1)}, bf16[128,1024]{1,0:T(8,128)(2,1)S(1)}, u32[]{:S(2)}, u32[]{:S(2)}) collective-permute-start(bf16[128,1024]{1,0:T(8,128)(2,1)S(1)} %fusion.1.rest_2_), channel_id=1, source_target_pairs={{0,32},{16,48},{32,0},{48,16},{64,96},{80,112},{96,64},{112,80},{1... | collective-permute-start | bytes 786440 | tf_op jit(solution)/shard_map/ppermute | solution.py:24
  133.3 17.4 %collective-permute-start.29 = (bf16[2,128,768]{2,1,0:T(8,128)(2,1)S(1)}, bf16[2,128,768]{2,1,0:T(8,128)(2,1)S(1)}, u32[]{:S(2)}, u32[]{:S(2)}) collective-permute-start(bf16[2,128,768]{2,1,0:T(8,128)(2,1)S(1)} %pad_maximum_fusion), channel_id=1, source_target_pairs={{0,48},{16,0},{32,16},{48,32},{64,112},{80,64},{96,80},{112,96},{1... | collective-permute-start | bytes 1179656 | tf_op jit(solution)/shard_map/ppermute | solution.py:24
  135.1 10.7 %collective-permute-start.31 = (bf16[128,1024]{1,0:T(8,128)(2,1)S(1)}, bf16[128,1024]{1,0:T(8,128)(2,1)S(1)}, u32[]{:S(2)}, u32[]{:S(2)}) collective-permute-start(bf16[128,1024]{1,0:T(8,128)(2,1)S(1)} %collective-permute-done.30.rest_1_), channel_id=1, source_target_pairs={{0,64},{16,80},{32,96},{48,112},{64,0},{80,16},{96,32},{112,48},{1... | collective-permute-start | bytes 786440 | tf_op jit(solution)/shard_map/ppermute | solution.py:24
  136.4 16.3 %collective-permute-start.26 = (bf16[2,128,768]{2,1,0:T(8,128)(2,1)S(1)}, bf16[2,128,768]{2,1,0:T(8,128)(2,1)S(1)}, u32[]{:S(2)}, u32[]{:S(2)}) collective-permute-start(bf16[2,128,768]{2,1,0:T(8,128)(2,1)S(1)} %pad_maximum_fusion), channel_id=1, source_target_pairs={{0,16},{16,32},{32,48},{48,0},{64,80},{80,96},{96,112},{112,64},{1... | collective-permute-start | bytes 1179656 | tf_op jit(solution)/shard_map/ppermute | solution.py:24
  136.6 19.6 %collective-permute-start.15 = (bf16[2,128,768]{2,1,0:T(8,128)(2,1)S(1)}, bf16[2,128,768]{2,1,0:T(8,128)(2,1)S(1)}, u32[]{:S(2)}, u32[]{:S(2)}) collective-permute-start(bf16[2,128,768]{2,1,0:T(8,128)(2,1)S(1)} %pad_maximum_fusion), channel_id=1, source_target_pairs={{0,32},{16,48},{32,0},{48,16},{64,96},{80,112},{96,64},{112,80},{1... | collective-permute-start | bytes 1179656 | tf_op jit(solution)/shard_map/ppermute | solution.py:24
  142.4 10.2 %collective-permute-start.28 = (bf16[128,1024]{1,0:T(8,128)(2,1)S(1)}, bf16[128,1024]{1,0:T(8,128)(2,1)S(1)}, u32[]{:S(2)}, u32[]{:S(2)}) collective-permute-start(bf16[128,1024]{1,0:T(8,128)(2,1)S(1)} %collective-permute-done.27.rest_1_), channel_id=1, source_target_pairs={{0,64},{16,80},{32,96},{48,112},{64,0},{80,16},{96,32},{112,48},{1... | collective-permute-start | bytes 786440 | tf_op jit(solution)/shard_map/ppermute | solution.py:24
  145.8 8.9 %collective-permute-start.24 = (bf16[128,1024]{1,0:T(8,128)(2,1)S(1)}, bf16[128,1024]{1,0:T(8,128)(2,1)S(1)}, u32[]{:S(2)}, u32[]{:S(2)}) collective-permute-start(bf16[128,1024]{1,0:T(8,128)(2,1)S(1)} %collective-permute-done.23.rest_1_), channel_id=1, source_target_pairs={{0,64},{16,80},{32,96},{48,112},{64,0},{80,16},{96,32},{112,48},{1... | collective-permute-start | bytes 786440 | tf_op jit(solution)/shard_map/ppermute | solution.py:24

commit v4 on v3

--- a/solution.py
+++ b/solution.py
@@ -12,7 +12,7 @@
 SEQ = ("xh", "z", "c")
 SHAPE = {"xh": 2, "z": 4, "c": 2, "y": 4, "xl": 2}
 STEPS = (1, 3, 2, 0)
-PEERS = ((0, 3), (1, 3), (0, 1), (1, 1), (0, 2), (1, 2), (1, 0))
+PEERS = ((0, 3), (0, 1), (1, 3), (1, 1), (0, 2), (1, 2), (1, 0))
 BF16, F32 = jnp.bfloat16, jnp.float32
 
 
@@ -24,108 +24,172 @@
     return lax.ppermute(x, CHIPS, pairs)
 
 
-def conv_norm(place, tokens, edge, conv_weight, gain):
+def conv_rows(ext, tok, cw, gn, conv, emit, place):
+    step, width = tok.shape
+    taps = cw.shape[0]
+    lanes = 512
+    pad = ext.shape[0] - step
+    group = width // 8
+    ext[pad:] = tok.astype(F32)
+    squares = jnp.zeros((step, 128), F32)
+    for p in range(width // lanes):
+        at = slice(p * lanes, (p + 1) * lanes)
+        acc = cw[0:1, at] * ext[pad : pad + step, at]
+        for k in range(1, taps):
+            acc = acc + cw[k : k + 1, at] * ext[pad - k : pad - k + step, at]
+        conv[:, at] = acc
+        for j in range(lanes // 128):
+            piece = acc[:, j * 128 : (j + 1) * 128]
+            squares = squares + piece * piece
+    mean = jnp.sum(squares, axis=1, keepdims=True) * (1.0 / width)
+    scale = lax.rsqrt(mean + 1e-05)
+    for p in range(8):
+        dx, dz = p // 4, p % 4
+        peer = (place[1] + dx) % 2 * 4 + (place[2] + dz) % 4
+        at = pl.ds(pl.multiple_of(peer * group, group), group)
+        emit(p, (conv[:, at] * scale * gn[:, at]).astype(BF16))
+
+
+STEP, PAD = 16, 8
+
+
+def conv_main(place, tokens, conv_weight, gain):
     rows, width = tokens.shape
-    taps = conv_weight.shape[0]
-    peers = 8
-    group = width // peers
-    step = 16
-    lanes = 512
-    pad = edge.shape[0]
-
-    def body(at_ref, tok, edg, cw, gn, *rest):
-        outs, (ext, conv) = rest[:peers], rest[peers:]
-        i = pl.program_id(0)
-
-        @pl.when(i == 0)
-        def _():
-            ext[:pad] = edg[...].astype(F32)
-
-        @pl.when(i > 0)
-        def _():
-            ext[:pad] = ext[step : step + pad]
-
-        ext[pad:] = tok[...].astype(F32)
-        squares = jnp.zeros((step, 128), F32)
-        for p in range(width // lanes):
-            at = slice(p * lanes, (p + 1) * lanes)
-            acc = cw[0:1, at] * ext[pad : pad + step, at]
-            for k in range(1, taps):
-                acc = acc + cw[k : k + 1, at] * ext[pad - k : pad - k + step, at]
-            conv[:, at] = acc
-            for j in range(lanes // 128):
-                piece = acc[:, j * 128 : (j + 1) * 128]
-                squares = squares + piece * piece
-        mean = jnp.sum(squares, axis=1, keepdims=True) * (1.0 / width)
-        scale = lax.rsqrt(mean + 1e-05)
-        for p in range(peers):
-            dx, dz = p // 4, p % 4
-            peer = (at_ref[1] + dx) % 2 * 4 + (at_ref[2] + dz) % 4
-            at = pl.ds(pl.multiple_of(peer * group, group), group)
-            outs[p][...] = (conv[:, at] * scale * gn[:, at]).astype(BF16)
-
+    tiles = rows // STEP
+
+    def body(at_ref, tok_h, cw_h, gn_h, *rest):
+        outs, (tok, cw, gn, ext, conv, sems) = rest[:8], rest[8:]
+        weights = pltpu.make_async_copy(cw_h, cw, sems.at[tiles])
+        gains = pltpu.make_async_copy(gn_h, gn, sems.at[tiles + 1])
+
+        def load(i):
+            at = pl.ds(pl.multiple_of(i * STEP, STEP), STEP)
+            return pltpu.make_async_copy(tok_h.at[at], tok.at[at], sems.at[i])
+
+        for i in range(2):
+            load(i).start()
+        weights.start()
+        gains.start()
+        for i in range(2, tiles):
+            load(i).start()
+        load(0).wait()
+        ext[:PAD] = tok[:STEP].astype(F32)[STEP - PAD :]
+        weights.wait()
+        gains.wait()
+
+        def tile(i, _):
+            load(i).wait()
+            at = pl.ds(pl.multiple_of(i * STEP, STEP), STEP)
+
+            def emit(p, value):
+                outs[p][at, :] = value
+
+            conv_rows(ext, tok[at, :], cw, gn, conv, emit, at_ref)
+            ext[:PAD] = ext[STEP : STEP + PAD]
+            return 0
+
+        lax.fori_loop(1, tiles, tile, 0)
+
+    hbm = pl.BlockSpec(memory_space=pltpu.HBM)
+    vmem = pl.BlockSpec(memory_space=pltpu.VMEM)
+    block = jax.ShapeDtypeStruct((rows, width // 8), BF16)
+    kept = [jax.ShapeDtypeStruct(a.shape, a.dtype) for a in (tokens, conv_weight, gain)]
     return pl.pallas_call(
         body,
-        grid_spec=pltpu.PrefetchScalarGridSpec(
-            num_scalar_prefetch=1,
-            grid=(rows // step,),
-            in_specs=[
-                pl.BlockSpec((step, width), lambda i, s: (i, 0)),
-                pl.BlockSpec((pad, width), lambda i, s: (0, 0)),
-                pl.BlockSpec((taps, width), lambda i, s: (0, 0)),
-                pl.BlockSpec((1, width), lambda i, s: (0, 0)),
-            ],
-            out_specs=[pl.BlockSpec((step, group), lambda i, s: (i, 0))] * peers,
-            scratch_shapes=[pltpu.VMEM((pad + step, width), F32), pltpu.VMEM((step, width), F32)],
-        ),
-        out_shape=[jax.ShapeDtypeStruct((rows, group), BF16)] * peers,
-        compiler_params=pltpu.CompilerParams(dimension_semantics=("arbitrary",), vmem_limit_bytes=12 * 2**20),
+        in_specs=[pl.BlockSpec(memory_space=pltpu.SMEM), hbm, hbm, hbm],
+        out_specs=[vmem] * 11,
+        out_shape=[block] * 8 + kept,
+        scratch_shapes=[
+            pltpu.VMEM((PAD + STEP, width), F32),
+            pltpu.VMEM((STEP, width), F32),
+            pltpu.SemaphoreType.DMA((tiles + 2,)),
+        ],
+        compiler_params=pltpu.CompilerParams(vmem_limit_bytes=16 * 2**20),
         cost_estimate=pl.CostEstimate(flops=4000000000, bytes_accessed=4 * rows * width, transcendentals=0),
-        name="conv_norm",
-    )(place, tokens, edge, conv_weight, gain)
-
-
-def gate_up(place, near, far, own_gate, other_gate, own_up, other_up):
+        name="conv_main",
+    )(place, *[pltpu.with_memory_space_constraint(a, pltpu.HBM) for a in (tokens, conv_weight, gain)])
+
+
+def conv_head(place, edge, tokens, conv_weight, gain, blocks):
+    width = tokens.shape[1]
+
+    def body(at_ref, edg, tok, cw, gn, *rest):
+        outs, (ext, conv, tile, sems) = rest[8:16], rest[16:]
+        ext[:PAD] = edg[...].astype(F32)
+        copies = []
+
+        def emit(p, value):
+            tile[p] = value
+            copies.append(pltpu.make_async_copy(tile.at[p], outs[p].at[pl.ds(0, STEP)], sems.at[p]))
+            copies[-1].start()
+
+        conv_rows(ext, tok[:STEP, :], cw, gn, conv, emit, at_ref)
+        for copy in copies:
+            copy.wait()
+
+    vmem = pl.BlockSpec(memory_space=pltpu.VMEM)
+    anywhere = pl.BlockSpec(memory_space=pl.ANY)
+    return pl.pallas_call(
+        body,
+        in_specs=[pl.BlockSpec(memory_space=pltpu.SMEM)] + [vmem] * 4 + [anywhere] * 8,
+        out_specs=[anywhere] * 8,
+        out_shape=[jax.ShapeDtypeStruct(b.shape, b.dtype) for b in blocks],
+        input_output_aliases={5 + i: i for i in range(8)},
+        scratch_shapes=[
+            pltpu.VMEM((PAD + STEP, width), F32),
+            pltpu.VMEM((STEP, width), F32),
+            pltpu.VMEM((8, STEP, width // 8), BF16),
+            pltpu.SemaphoreType.DMA((8,)),
+        ],
+        compiler_params=pltpu.CompilerParams(vmem_limit_bytes=16 * 2**20),
+        cost_estimate=pl.CostEstimate(flops=400000000, bytes_accessed=4 * STEP * width, transcendentals=0),
+        name="conv_head",
+    )(place, edge, tokens, conv_weight, gain, *blocks)
+
+
+CUT = 768
+
+
+def gate_up(place, near, far, own_gate, other_gate, own_up, other_up, lo, hi, joined):
     per, depth = near.shape
-    half, cols = own_gate.shape
+    half = own_gate.shape[0]
     tile = 256
-    first = 3
-
-    def body(at_ref, near_ref, far_ref, g0, g1, u0, u1, one, two_near, two_far):
+
+    def body(at_ref, near_ref, far_ref, g0, g1, u0, u1, *outs):
         c = at_ref[0]
         mine = pl.ds(pl.multiple_of(c * half, half), half)
         theirs = pl.ds(pl.multiple_of((1 - c) * half, half), half)
-
         x_mine = jnp.concatenate([near_ref[:, mine], far_ref[:, mine]], 0)
         x_theirs = jnp.concatenate([near_ref[:, theirs], far_ref[:, theirs]], 0)
-
-        def product(at, own, other):
-            total = jnp.dot(x_mine, own[:, at], preferred_element_type=F32) + jnp.dot(
-                x_theirs, other[:, at], preferred_element_type=F32
-            )
-            return total.astype(BF16)
-
-        split = first * tile
         for k, (a, b) in enumerate(((g0, g1), (u0, u1))):
-            for n in range(0, cols, tile):
-                total = product(slice(n, n + tile), a, b)
-                if n < split:
-                    one[0, k, :, n : n + tile] = total[:per]
-                    one[1, k, :, n : n + tile] = total[per:]
+            for n in range(lo, hi, tile):
+                at = slice(n, n + tile)
+                total = jnp.dot(x_mine, a[:, at], preferred_element_type=F32) + jnp.dot(
+                    x_theirs, b[:, at], preferred_element_type=F32
+                )
+                total = total.astype(BF16)
+                to = slice(n - lo, n - lo + tile)
+                if joined:
+                    outs[0][0, k, :, to] = total[:per]
+                    outs[0][1, k, :, to] = total[per:]
                 else:
-                    two_near[k, :, n - split : n - split + tile] = total[:per]
-                    two_far[k, :, n - split : n - split + tile] = total[per:]
+                    outs[0][k, :, to] = total[:per]
+                    outs[1][k, :, to] = total[per:]
 
     vmem = pl.BlockSpec(memory_space=pltpu.VMEM)
-    two_shape = jax.ShapeDtypeStruct((2, per, cols - first * tile), BF16)
+    width = hi - lo
+    if joined:
+        shapes = [jax.ShapeDtypeStruct((2, 2, per, width), BF16)]
+    else:
+        shapes = [jax.ShapeDtypeStruct((2, per, width), BF16)] * 2
     return pl.pallas_call(
         body,
         in_specs=[pl.BlockSpec(memory_space=pltpu.SMEM)] + [vmem] * 6,
-        out_specs=[vmem] * 3,
-        out_shape=[jax.ShapeDtypeStruct((2, 2, per, first * tile), BF16), two_shape, two_shape],
+        out_specs=[vmem] * len(shapes),
+        out_shape=shapes,
         compiler_params=pltpu.CompilerParams(vmem_limit_bytes=24 * 2**20),
         cost_estimate=pl.CostEstimate(
-            flops=8 * per * depth * cols, bytes_accessed=8 * half * cols, transcendentals=0
+            flops=8 * per * depth * width, bytes_accessed=8 * half * width, transcendentals=0
         ),
         name="gate_up",
     )(place, near, far, own_gate, other_gate, own_up, other_up)
@@ -202,16 +266,20 @@
     gate_other = swap(gate_weight)
     up_other = swap(up_weight)
     down_other = swap(down_weight)
-    normed = conv_norm(place, tokens, edge, conv_weight, norm_gain[None, :])
+    *normed, held, taps, gain = conv_main(place, tokens, conv_weight, norm_gain[None, :])
+    normed = conv_head(place, edge, held, taps, gain, normed)
     rows = {(0, 0): normed[0]}
     for dx, dz in PEERS:
         rows[dx, -dz % 4] = hop(normed[dx * 4 + dz], dx, dz)
     one, near, far, one_in, far_in = {}, {}, {}, {}, {}
+    weights = (gate_weight, gate_other, up_weight, up_other)
+    cols = gate_weight.shape[1]
     for e in STEPS:
-        one[e], near[e], far[e] = gate_up(place, rows[0, e], rows[1, e], gate_weight, gate_other, up_weight, up_other)
-        far_in[e] = hop(far[e], 1, 0)
+        (one[e],) = gate_up(place, rows[0, e], rows[1, e], *weights, 0, CUT, True)
         if e:
             one_in[e] = hop(one[e], 0, e)
+        near[e], far[e] = gate_up(place, rows[0, e], rows[1, e], *weights, CUT, cols, False)
+        far_in[e] = hop(far[e], 1, 0)
     two_in = {}
     for e in STEPS[:3]:
         both = total(near[e], far_in[e]).astype(BF16)

time: 201 us -> 207 us (1.030)
  the two profiles are of different devices: /device:TPU:0 before, /device:TPU:1 now
where the time goes in v4:
time: 207 us; the launch traced here: 203 us
  starting transfers between devices  66.2 us (32%)
  waiting for transfers between devices  54.3 us (26%)
  blocking collectives  41.7 us (20%)
  Pallas kernels  36 us (17%)
  other arithmetic  2.33 us (1%)
    ppermute x29, waiting for transfers between devices, hop(): return lax.ppermute(x, CHIPS, pairs)  54.3 us
    ppermute x29, starting transfers between devices, hop(): return lax.ppermute(x, CHIPS, pairs)  52.4 us
    all_to_all x1, blocking collectives, shards(): arrived = lax.all_to_all(terms, TP, split_axis=0, concat_axis=0, tiled=True)  25.4 us
    pallas_call x8, Pallas kernels, gate_up(): pl.pallas_call(body, in_specs=[pl.BlockSpec(memory_space=pltpu.SMEM)] + [...  21.1 us
    all_to_all x1, blocking collectives, shards(): out = lax.all_to_all(summed, CHIPS, split_axis=0, concat_axis=0, tiled=True)  16.3 us
    ppermute x3, starting transfers between devices, shards(): swap = lambda w: lax.ppermute(w, 'c', [(0, 1), (1, 0)])  9.74 us
    pallas_call x4, Pallas kernels, down(): pl.pallas_call(body, grid_spec=pltpu.PrefetchScalarGridSpec(num_scalar_pr...  7.95 us
    pallas_call x1, Pallas kernels, conv_main(): pl.pallas_call(body, in_specs=[pl.BlockSpec(memory_space=pltpu.SMEM), hbm...  5.4 us
  transfers between devices with their start and end apart: 33, of which 14 were waited for; matrix products, arithmetic and copies ran while one was open for 1% of the time, Pallas kernels for 17%

profile of v4, /device:TPU:1, one launch (start us, length us, event | category | flops | bytes accessed | tf_op | source)
XLA Modules:
  0.0 202.6 jit_solution(15463588534327989325)
XLA Ops:
  0.0 1.4 collective-permute-start.2
  2.3 4.0 %collective-permute-start = (bf16[8,8192]{1,0:T(8,128)(2,1)S(1)}, bf16[8,8192]{1,0:T(8,128)(2,1)S(1)}, u32[]{:S(2)}, u32[]{:S(2)}) collective-permute-start(bf16[8,8192]{1,0:T(8,128)(2,1)S(1)} %slice.39), channel_id=1, source_target_pairs={{0,8},{8,16},{16,24},{24,32},{32,40},{40,48},{48,56},{56,64},{64,7... | collective-permute-start | bytes 393224 | tf_op jit(solution)/shard_map/ppermute | solution.py:265
  6.4 5.4 %conv_main.1 = (bf16[128,1024]{1,0:T(8,128)(2,1)S(1)}, bf16[128,1024]{1,0:T(8,128)(2,1)S(1)}, bf16[128,1024]{1,0:T(8,128)(2,1)S(1)}, bf16[128,1024]{1,0:T(8,128)...) custom-call(s32[3]{0:T(128)S(1)} %pad_add_fusion.at_ref, ...), custom_call_target="tpu_custom_call" | custom-call | flops 4000000000 | bytes 4194304 | tf_op jit(solution)/shard_map/conv_main/pallas_call | solution.py:97
  11.9 1.6 conv_head.1
  13.5 3.5 %collective-permute-start.4 = (bf16[128,1024]{1,0:T(8,128)(2,1)S(1)}, bf16[128,1024]{1,0:T(8,128)(2,1)S(1)}, u32[]{:S(2)}, u32[]{:S(2)}) collective-permute-start(bf16[128,1024]{1,0:T(8,128)(2,1)S(1)} %get-tuple-element.45), channel_id=1, source_target_pairs={{0,48},{16,0},{32,16},{48,32},{64,112},{80,64},{96,80},{112,96},{1... | collective-permute-start | bytes 786440 | tf_op jit(solution)/shard_map/ppermute | solution.py:24
  17.1 2.6 %collective-permute-start.5 = (bf16[128,1024]{1,0:T(8,128)(2,1)S(1)}, bf16[128,1024]{1,0:T(8,128)(2,1)S(1)}, u32[]{:S(2)}, u32[]{:S(2)}) collective-permute-start(bf16[128,1024]{1,0:T(8,128)(2,1)S(1)} %get-tuple-element.46), channel_id=1, source_target_pairs={{0,112},{16,64},{32,80},{48,96},{64,48},{80,0},{96,16},{112,32},{1... | collective-permute-start | bytes 786440 | tf_op jit(solution)/shard_map/ppermute | solution.py:24
  19.6 8.4 %collective-permute-done.4.near_ref = bf16[128,1024]{1,0:T(8,128)(2,1)S(1)} collective-permute-done((bf16[128,1024]{1,0:T(8,128)(2,1)S(1)}, bf16[128,1024]{1,0:T(8,128)(2,1)S(1)}, u32[]{:S(2)}, u32[]{:S(2)}) %collective-permute-start.4) | collective-permute-done | bytes 262176 | tf_op jit(solution)/shard_map/ppermute | solution.py:24
  28.0 2.2 %collective-permute-start.8 = (bf16[128,1024]{1,0:T(8,128)(2,1)S(1)}, bf16[128,1024]{1,0:T(8,128)(2,1)S(1)}, u32[]{:S(2)}, u32[]{:S(2)}) collective-permute-start(bf16[128,1024]{1,0:T(8,128)(2,1)S(1)} %get-tuple-element.48), channel_id=1, source_target_pairs={{0,80},{16,96},{32,112},{48,64},{64,16},{80,32},{96,48},{112,0},{1... | collective-permute-start | bytes 786440 | tf_op jit(solution)/shard_map/ppermute | solution.py:24
  30.3 1.5 collective-permute-start.10
  31.8 3.0 %collective-permute-start.11 = (bf16[128,1024]{1,0:T(8,128)(2,1)S(1)}, bf16[128,1024]{1,0:T(8,128)(2,1)S(1)}, u32[]{:S(2)}, u32[]{:S(2)}) collective-permute-start(bf16[128,1024]{1,0:T(8,128)(2,1)S(1)} %get-tuple-element.50), channel_id=1, source_target_pairs={{0,96},{16,112},{32,64},{48,80},{64,32},{80,48},{96,0},{112,16},{1... | collective-permute-start | bytes 786440 | tf_op jit(solution)/shard_map/ppermute | solution.py:24
  35.9 2.8 %gate_up.13 = (bf16[2,128,1024]{2,1,0:T(8,128)(2,1)S(1)}, bf16[2,128,1024]{2,1,0:T(8,128)(2,1)S(1)}) custom-call(s32[3]{0:T(128)S(1)} %pad_add_fusion.at_ref, bf16[128,1024]{1,0:T(8,128)(2,1)S(1)} %collective-permute-done.4.near_ref, bf16[128,1024]{1,0:T(8,128)(2,1)S(1)} %collective-permute-done.5.far_ref, bf16[512,1792]{1,0:T(8,128)(2,1)S(1)} %copy-done, ...), custom_call_target="tpu_custom_call" | custom-call | flops 1073741824 | bytes 4194304 | tf_op jit(solution)/shard_map/gate_up/pallas_call | solution.py:185
  38.7 1.9 collective-permute-start.17
  41.1 2.8 %gate_up.14 = (bf16[2,128,1024]{2,1,0:T(8,128)(2,1)S(1)}, bf16[2,128,1024]{2,1,0:T(8,128)(2,1)S(1)}) custom-call(s32[3]{0:T(128)S(1)} %pad_add_fusion.at_ref, bf16[128,1024]{1,0:T(8,128)(2,1)S(1)} %collective-permute-done.7.near_ref, bf16[128,1024]{1,0:T(8,128)(2,1)S(1)} %collective-permute-done.8.far_ref, bf16[512,1792]{1,0:T(8,128)(2,1)S(1)} %copy-done, ...), custom_call_target="tpu_custom_call" | custom-call | flops 1073741824 | bytes 4194304 | tf_op jit(solution)/shard_map/gate_up/pallas_call | solution.py:185
  44.6 5.9 %collective-permute-done.10.near_ref = bf16[128,1024]{1,0:T(8,128)(2,1)S(1)} collective-permute-done((bf16[128,1024]{1,0:T(8,128)(2,1)S(1)}, bf16[128,1024]{1,0:T(8,128)(2,1)S(1)}, u32[]{:S(2)}, u32[]{:S(2)}) %collective-permute-start.10) | collective-permute-done | bytes 262176 | tf_op jit(solution)/shard_map/ppermute | solution.py:24
  50.5 2.8 %gate_up.15 = (bf16[2,128,1024]{2,1,0:T(8,128)(2,1)S(1)}, bf16[2,128,1024]{2,1,0:T(8,128)(2,1)S(1)}) custom-call(s32[3]{0:T(128)S(1)} %pad_add_fusion.at_ref, bf16[128,1024]{1,0:T(8,128)(2,1)S(1)} %collective-permute-done.10.near_ref, bf16[128,1024]{1,0:T(8,128)(2,1)S(1)} %collective-permute-done.11.far_ref, bf16[512,1792]{1,0:T(8,128)(2,1)S(1)} %copy-done, ...), custom_call_target="tpu_custom_call" | custom-call | flops 1073741824 | bytes 4194304 | tf_op jit(solution)/shard_map/gate_up/pallas_call | solution.py:185
  53.3 2.5 %collective-permute-start.21 = (bf16[2,128,1024]{2,1,0:T(8,128)(2,1)S(1)}, bf16[2,128,1024]{2,1,0:T(8,128)(2,1)S(1)}, u32[]{:S(2)}, u32[]{:S(2)}) collective-permute-start(bf16[2,128,1024]{2,1,0:T(8,128)(2,1)S(1)} %get-tuple-element.58), channel_id=1, source_target_pairs={{0,64},{16,80},{32,96},{48,112},{64,0},{80,16},{96,32},{112,48},{1... | collective-permute-start | bytes 1572872 | tf_op jit(solution)/shard_map/ppermute | solution.py:24
  55.8 2.5 %gate_up.9 = bf16[2,2,128,768]{3,2,1,0:T(8,128)(2,1)S(1)} custom-call(s32[3]{0:T(128)S(1)} %pad_add_fusion.at_ref, bf16[128,1024]{1,0:T(8,128)(2,1)S(1)} %collective-permute-done.4.near_ref, bf16[128,1024]{1,0:T(8,128)(2,1)S(1)} %collective-permute-done.5.far_ref, bf16[512,1792]{1,0:T(8,128)(2,1)S(1)} %copy-done, ...), custom_call_target="tpu_custom_call" | custom-call | flops 805306368 | bytes 3145728 | tf_op jit(solution)/shard_map/gate_up/pallas_call | solution.py:185
  58.4 2.5 %gate_up.10 = bf16[2,2,128,768]{3,2,1,0:T(8,128)(2,1)S(1)} custom-call(s32[3]{0:T(128)S(1)} %pad_add_fusion.at_ref, bf16[128,1024]{1,0:T(8,128)(2,1)S(1)} %collective-permute-done.7.near_ref, bf16[128,1024]{1,0:T(8,128)(2,1)S(1)} %collective-permute-done.8.far_ref, bf16[512,1792]{1,0:T(8,128)(2,1)S(1)} %copy-done, ...), custom_call_target="tpu_custom_call" | custom-call | flops 805306368 | bytes 3145728 | tf_op jit(solution)/shard_map/gate_up/pallas_call | solution.py:185
  60.9 2.5 %gate_up.11 = bf16[2,2,128,768]{3,2,1,0:T(8,128)(2,1)S(1)} custom-call(s32[3]{0:T(128)S(1)} %pad_add_fusion.at_ref, bf16[128,1024]{1,0:T(8,128)(2,1)S(1)} %collective-permute-done.10.near_ref, bf16[128,1024]{1,0:T(8,128)(2,1)S(1)} %collective-permute-done.11.far_ref, bf16[512,1792]{1,0:T(8,128)(2,1)S(1)} %copy-done, ...), custom_call_target="tpu_custom_call" | custom-call | flops 805306368 | bytes 3145728 | tf_op jit(solution)/shard_map/gate_up/pallas_call | solution.py:185
  63.4 2.7 %collective-permute-start.9 = (bf16[2,2,128,768]{3,2,1,0:T(8,128)(2,1)S(1)}, bf16[2,2,128,768]{3,2,1,0:T(8,128)(2,1)S(1)}, u32[]{:S(2)}, u32[]{:S(2)}) collective-permute-start(bf16[2,2,128,768]{3,2,1,0:T(8,128)(2,1)S(1)} %gate_up.10), channel_id=1, source_target_pairs={{0,48},{16,0},{32,16},{48,32},{64,112},{80,64},{96,80},{112,96},{1... | collective-permute-start | bytes 2359304 | tf_op jit(solution)/shard_map/ppermute | solution.py:24
  66.1 2.8 %gate_up.12 = (bf16[2,128,1024]{2,1,0:T(8,128)(2,1)S(1)}, bf16[2,128,1024]{2,1,0:T(8,128)(2,1)S(1)}) custom-call(s32[3]{0:T(128)S(1)} %pad_add_fusion.at_ref, bf16[128,1024]{1,0:T(8,128)(2,1)S(1)} %get-tuple-element.43.near_ref, bf16[128,1024]{1,0:T(8,128)(2,1)S(1)} %collective-permute-done.1.far_ref, bf16[512,1792]{1,0:T(8,128)(2,1)S(1)} %copy-done, ...), custom_call_target="tpu_custom_call" | custom-call | flops 1073741824 | bytes 4194304 | tf_op jit(solution)/shard_map/gate_up/pallas_call | solution.py:185
  70.4 3.7 %collective-permute-start.16 = (bf16[2,128,1024]{2,1,0:T(8,128)(2,1)S(1)}, bf16[2,128,1024]{2,1,0:T(8,128)(2,1)S(1)}, u32[]{:S(2)}, u32[]{:S(2)}) collective-permute-start(bf16[2,128,1024]{2,1,0:T(8,128)(2,1)S(1)} %get-tuple-element.52), channel_id=1, source_target_pairs={{0,64},{16,80},{32,96},{48,112},{64,0},{80,16},{96,32},{112,48},{1... | collective-permute-start | bytes 1572872 | tf_op jit(solution)/shard_map/ppermute | solution.py:24
  74.3 7.3 %collective-permute-done.21 = bf16[2,128,1024]{2,1,0:T(8,128)(2,1)S(1)} collective-permute-done((bf16[2,128,1024]{2,1,0:T(8,128)(2,1)S(1)}, bf16[2,128,1024]{2,1,0:T(8,128)(2,1)S(1)}, u32[]{:S(2)}, u32[]{:S(2)}) %collective-permute-start.21) | collective-permute-done | bytes 524320 | tf_op jit(solution)/shard_map/ppermute | solution.py:24
  81.6 1.6 collective-permute-start.18
  83.4 3.2 %collective-permute-start.20 = (bf16[2,128,1024]{2,1,0:T(8,128)(2,1)S(1)}, bf16[2,128,1024]{2,1,0:T(8,128)(2,1)S(1)}, u32[]{:S(2)}, u32[]{:S(2)}) collective-permute-start(bf16[2,128,1024]{2,1,0:T(8,128)(2,1)S(1)} %add_convert_fusion.1), channel_id=1, source_target_pairs={{0,48},{16,0},{32,16},{48,32},{64,112},{80,64},{96,80},{112,96},{1... | collective-permute-start | bytes 1572872 | tf_op jit(solution)/shard_map/ppermute | solution.py:24
  86.6 1.6 collective-permute-start.22
  88.2 5.6 %collective-permute-done.12 = bf16[2,2,128,768]{3,2,1,0:T(8,128)(2,1)S(1)} collective-permute-done((bf16[2,2,128,768]{3,2,1,0:T(8,128)(2,1)S(1)}, bf16[2,2,128,768]{3,2,1,0:T(8,128)(2,1)S(1)}, u32[]{:S(2)}, u32[]{:S(2)}) %collective-permute-start.12) | collective-permute-done | bytes 786464 | tf_op jit(solution)/shard_map/ppermute | solution.py:24
  93.8 8.4 %collective-permute-start.25 = (bf16[1792,512]{1,0:T(8,128)(2,1)S(1)}, bf16[1792,512]{1,0:T(8,128)(2,1)S(1)}, u32[]{:S(2)}, u32[]{:S(2)}) collective-permute-start(bf16[1792,512]{1,0:T(8,128)(2,1)S(1)} %copy-done.2), channel_id=1, source_target_pairs={{0,8},{8,0},{1,9},{9,1},{2,10},{10,2},{3,11},{11,3},{4,12},{12,4},... | collective-permute-start | bytes 5505032 | tf_op jit(solution)/shard_map/ppermute | solution.py:264
  102.2 2.5 %gate_up.8 = bf16[2,2,128,768]{3,2,1,0:T(8,128)(2,1)S(1)} custom-call(s32[3]{0:T(128)S(1)} %pad_add_fusion.at_ref, bf16[128,1024]{1,0:T(8,128)(2,1)S(1)} %get-tuple-element.43.near_ref, bf16[128,1024]{1,0:T(8,128)(2,1)S(1)} %collective-permute-done.1.far_ref, bf16[512,1792]{1,0:T(8,128)(2,1)S(1)} %copy-done, ...), custom_call_target="tpu_custom_call" | custom-call | flops 805306368 | bytes 3145728 | tf_op jit(solution)/shard_map/gate_up/pallas_call | solution.py:185
  105.4 1.6 collective-permute-done.18
  107.0 3.9 %collective-permute-done.20 = bf16[2,128,1024]{2,1,0:T(8,128)(2,1)S(1)} collective-permute-done((bf16[2,128,1024]{2,1,0:T(8,128)(2,1)S(1)}, bf16[2,128,1024]{2,1,0:T(8,128)(2,1)S(1)}, u32[]{:S(2)}, u32[]{:S(2)}) %collective-permute-start.20) | collective-permute-done | bytes 524320 | tf_op jit(solution)/shard_map/ppermute | solution.py:24
  111.0 5.4 %collective-permute-done.22 = bf16[2,128,1024]{2,1,0:T(8,128)(2,1)S(1)} collective-permute-done((bf16[2,128,1024]{2,1,0:T(8,128)(2,1)S(1)}, bf16[2,128,1024]{2,1,0:T(8,128)(2,1)S(1)}, u32[]{:S(2)}, u32[]{:S(2)}) %collective-permute-start.22) | collective-permute-done | bytes 524320 | tf_op jit(solution)/shard_map/ppermute | solution.py:24
  117.2 7.2 %collective-permute-start.30 = (bf16[128,1024]{1,0:T(8,128)(2,1)S(1)}, bf16[128,1024]{1,0:T(8,128)(2,1)S(1)}, u32[]{:S(2)}, u32[]{:S(2)}) collective-permute-start(bf16[128,1024]{1,0:T(8,128)(2,1)S(1)} %fusion.1.rest_2_), channel_id=1, source_target_pairs={{0,48},{16,0},{32,16},{48,32},{64,112},{80,64},{96,80},{112,96},{1... | collective-permute-start | bytes 786440 | tf_op jit(solution)/shard_map/ppermute | solution.py:24
  124.7 3.0 %collective-permute-start.14 = (bf16[128,768]{1,0:T(8,128)(2,1)S(1)}, bf16[128,768]{1,0:T(8,128)(2,1)S(1)}, u32[]{:S(2)}, u32[]{:S(2)}) collective-permute-start(bf16[128,768]{1,0:T(8,128)(2,1)S(1)} %fusion.3.rest_0_), channel_id=1, source_target_pairs={{0,64},{16,80},{32,96},{48,112},{64,0},{80,16},{96,32},{112,48},{1... | collective-permute-start | bytes 589832 | tf_op jit(solution)/shard_map/ppermute | solution.py:24
  127.8 5.4 %collective-permute-done.14.rest_1_ = bf16[128,768]{1,0:T(8,128)(2,1)S(1)} collective-permute-done((bf16[128,768]{1,0:T(8,128)(2,1)S(1)}, bf16[128,768]{1,0:T(8,128)(2,1)S(1)}, u32[]{:S(2)}, u32[]{:S(2)}) %collective-permute-start.14) | collective-permute-done | bytes 196640 | tf_op jit(solution)/shard_map/ppermute | solution.py:24
  133.3 4.8 %collective-permute-start.29 = (bf16[2,128,768]{2,1,0:T(8,128)(2,1)S(1)}, bf16[2,128,768]{2,1,0:T(8,128)(2,1)S(1)}, u32[]{:S(2)}, u32[]{:S(2)}) collective-permute-start(bf16[2,128,768]{2,1,0:T(8,128)(2,1)S(1)} %pad_maximum_fusion), channel_id=1, source_target_pairs={{0,48},{16,0},{32,16},{48,32},{64,112},{80,64},{96,80},{112,96},{1... | collective-permute-start | bytes 1179656 | tf_op jit(solution)/shard_map/ppermute | solution.py:24
  138.3 1.8 collective-permute-start.15
  140.0 2.3 %collective-permute-start.28 = (bf16[128,1024]{1,0:T(8,128)(2,1)S(1)}, bf16[128,1024]{1,0:T(8,128)(2,1)S(1)}, u32[]{:S(2)}, u32[]{:S(2)}) collective-permute-start(bf16[128,1024]{1,0:T(8,128)(2,1)S(1)} %collective-permute-done.27.rest_1_), channel_id=1, source_target_pairs={{0,64},{16,80},{32,96},{48,112},{64,0},{80,16},{96,32},{112,48},{1... | collective-permute-start | bytes 786440 | tf_op jit(solution)/shard_map/ppermute | solution.py:24
  142.3 2.8 %collective-permute-done.31.rest_2_ = bf16[128,1024]{1,0:T(8,128)(2,1)S(1)} collective-permute-done((bf16[128,1024]{1,0:T(8,128)(2,1)S(1)}, bf16[128,1024]{1,0:T(8,128)(2,1)S(1)}, u32[]{:S(2)}, u32[]{:S(2)}) %collective-permute-start.31) | collective-permute-done | bytes 262176 | tf_op jit(solution)/shard_map/ppermute | solution.py:24
  145.1 2.0 down.4.rest_5_
  147.1 3.2 %collective-permute-done.29.rest_0_ = bf16[2,128,768]{2,1,0:T(8,128)(2,1)S(1)} collective-permute-done((bf16[2,128,768]{2,1,0:T(8,128)(2,1)S(1)}, bf16[2,128,768]{2,1,0:T(8,128)(2,1)S(1)}, u32[]{:S(2)}, u32[]{:S(2)}) %collective-permute-start.29) | collective-permute-done | bytes 393248 | tf_op jit(solution)/shard_map/ppermute | solution.py:24
  150.3 2.0 down.5.rest_5_
  152.3 2.0 down.6.rest_5_
  154.3 1.4 collective-permute-done.24.rest_2_
  155.6 2.1 %collective-permute-done.15.rest_0_ = bf16[2,128,768]{2,1,0:T(8,128)(2,1)S(1)} collective-permute-done((bf16[2,128,768]{2,1,0:T(8,128)(2,1)S(1)}, bf16[2,128,768]{2,1,0:T(8,128)(2,1)S(1)}, u32[]{:S(2)}, u32[]{:S(2)}) %collective-permute-start.15) | collective-permute-done | bytes 393248 | tf_op jit(solution)/shard_map/ppermute | solution.py:24
  157.8 2.0 down.7
  159.8 25.4 %all_to_all.10 = bf16[8,8,16,1024]{3,2,1,0:T(8,128)(2,1)S(1)} all-to-all(bf16[8,8,16,1024]{3,2,1,0:T(8,128)(2,1)S(1)} %down.7), channel_id=1, replica_groups=mesh['xh'=2,'z'=4,'c'=2,'y'=4,'xl'=2] {'y','xl'}, dimensions={0} | all-to-all | bytes 4194304 | tf_op jit(solution)/shard_map/all_to_all | solution.py:307
  185.6 16.3 %all_to_all.11 = bf16[8,16,1024]{2,1,0:T(8,128)(2,1)S(1)} all-to-all(bf16[8,16,1024]{2,1,0:T(8,128)(2,1)S(1)} %reduce_sum.12), channel_id=1, replica_groups=mesh['xh'=2,'z'=4,'c'=2,'y'=4,'xl'=2] {'xh','z'}, dimensions={0} | all-to-all | bytes 524288 | tf_op jit(solution)/shard_map/all_to_all | solution.py:309
  (54 shorter events, 8.6 us)
Async XLA Ops:
  0.0 31.8 %collective-permute-start.2 = (bf16[512,1792]{1,0:T(8,128)(2,1)}, bf16[512,1792]{1,0:T(8,128)(2,1)S(1)}, u32[]{:S(2)}, u32[]{:S(2)}) collective-permute-start(bf16[512,1792]{1,0:T(8,128)(2,1)} %g0.15), channel_id=1, source_target_pairs={{0,8},{8,0},{1,9},{9,1},{2,10},{10,2},{3,11},{11,3},{4,12},{12,4},... | collective-permute-start | bytes 5505032 | tf_op jit(solution)/shard_map/ppermute | solution.py:264
  1.4 33.4 %collective-permute-start.3 = (bf16[512,1792]{1,0:T(8,128)(2,1)}, bf16[512,1792]{1,0:T(8,128)(2,1)}, u32[]{:S(2)}, u32[]{:S(2)}) collective-permute-start(bf16[512,1792]{1,0:T(8,128)(2,1)} %u0.15), channel_id=1, source_target_pairs={{0,8},{8,0},{1,9},{9,1},{2,10},{10,2},{3,11},{11,3},{4,12},{12,4},... | collective-permute-start | bytes 5505032 | tf_op jit(solution)/shard_map/ppermute | solution.py:264
  2.3 9.6 %collective-permute-start = (bf16[8,8192]{1,0:T(8,128)(2,1)S(1)}, bf16[8,8192]{1,0:T(8,128)(2,1)S(1)}, u32[]{:S(2)}, u32[]{:S(2)}) collective-permute-start(bf16[8,8192]{1,0:T(8,128)(2,1)S(1)} %slice.39), channel_id=1, source_target_pairs={{0,8},{8,16},{16,24},{24,32},{32,40},{40,48},{48,56},{56,64},{64,7... | collective-permute-start | bytes 393224 | tf_op jit(solution)/shard_map/ppermute | solution.py:265
  11.9 24.1 %copy-start = (bf16[512,1792]{1,0:T(8,128)(2,1)S(1)}, bf16[512,1792]{1,0:T(8,128)(2,1)}, u32[]{:S(2)}) copy-start(bf16[512,1792]{1,0:T(8,128)(2,1)} %g0.15) | copy-start | bytes 5505028
  11.9 24.1 %copy-start.1 = (bf16[512,1792]{1,0:T(8,128)(2,1)S(1)}, bf16[512,1792]{1,0:T(8,128)(2,1)}, u32[]{:S(2)}) copy-start(bf16[512,1792]{1,0:T(8,128)(2,1)} %u0.15) | copy-start | bytes 5505028
  13.5 14.5 %collective-permute-start.4 = (bf16[128,1024]{1,0:T(8,128)(2,1)S(1)}, bf16[128,1024]{1,0:T(8,128)(2,1)S(1)}, u32[]{:S(2)}, u32[]{:S(2)}) collective-permute-start(bf16[128,1024]{1,0:T(8,128)(2,1)S(1)} %get-tuple-element.45), channel_id=1, source_target_pairs={{0,48},{16,0},{32,16},{48,32},{64,112},{80,64},{96,80},{112,96},{1... | collective-permute-start | bytes 786440 | tf_op jit(solution)/shard_map/ppermute | solution.py:24
  17.1 13.2 %collective-permute-start.5 = (bf16[128,1024]{1,0:T(8,128)(2,1)S(1)}, bf16[128,1024]{1,0:T(8,128)(2,1)S(1)}, u32[]{:S(2)}, u32[]{:S(2)}) collective-permute-start(bf16[128,1024]{1,0:T(8,128)(2,1)S(1)} %get-tuple-element.46), channel_id=1, source_target_pairs={{0,112},{16,64},{32,80},{48,96},{64,48},{80,0},{96,16},{112,32},{1... | collective-permute-start | bytes 786440 | tf_op jit(solution)/shard_map/ppermute | solution.py:24
  19.6 19.1 %collective-permute-start.7 = (bf16[128,1024]{1,0:T(8,128)(2,1)S(1)}, bf16[128,1024]{1,0:T(8,128)(2,1)S(1)}, u32[]{:S(2)}, u32[]{:S(2)}) collective-permute-start(bf16[128,1024]{1,0:T(8,128)(2,1)S(1)} %get-tuple-element.47), channel_id=1, source_target_pairs={{0,16},{16,32},{32,48},{48,0},{64,80},{80,96},{96,112},{112,64},{1... | collective-permute-start | bytes 786440 | tf_op jit(solution)/shard_map/ppermute | solution.py:24
  28.0 13.1 %collective-permute-start.8 = (bf16[128,1024]{1,0:T(8,128)(2,1)S(1)}, bf16[128,1024]{1,0:T(8,128)(2,1)S(1)}, u32[]{:S(2)}, u32[]{:S(2)}) collective-permute-start(bf16[128,1024]{1,0:T(8,128)(2,1)S(1)} %get-tuple-element.48), channel_id=1, source_target_pairs={{0,80},{16,96},{32,112},{48,64},{64,16},{80,32},{96,48},{112,0},{1... | collective-permute-start | bytes 786440 | tf_op jit(solution)/shard_map/ppermute | solution.py:24
  30.3 20.2 %collective-permute-start.10 = (bf16[128,1024]{1,0:T(8,128)(2,1)S(1)}, bf16[128,1024]{1,0:T(8,128)(2,1)S(1)}, u32[]{:S(2)}, u32[]{:S(2)}) collective-permute-start(bf16[128,1024]{1,0:T(8,128)(2,1)S(1)} %get-tuple-element.49), channel_id=1, source_target_pairs={{0,32},{16,48},{32,0},{48,16},{64,96},{80,112},{96,64},{112,80},{1... | collective-permute-start | bytes 786440 | tf_op jit(solution)/shard_map/ppermute | solution.py:24
  31.8 18.7 %collective-permute-start.11 = (bf16[128,1024]{1,0:T(8,128)(2,1)S(1)}, bf16[128,1024]{1,0:T(8,128)(2,1)S(1)}, u32[]{:S(2)}, u32[]{:S(2)}) collective-permute-start(bf16[128,1024]{1,0:T(8,128)(2,1)S(1)} %get-tuple-element.50), channel_id=1, source_target_pairs={{0,96},{16,112},{32,64},{48,80},{64,32},{80,48},{96,0},{112,16},{1... | collective-permute-start | bytes 786440 | tf_op jit(solution)/shard_map/ppermute | solution.py:24
  34.8 28.6 %collective-permute-start.1 = (bf16[128,1024]{1,0:T(8,128)(2,1)S(1)}, bf16[128,1024]{1,0:T(8,128)(2,1)S(1)}, u32[]{:S(2)}, u32[]{:S(2)}) collective-permute-start(bf16[128,1024]{1,0:T(8,128)(2,1)S(1)} %get-tuple-element.44), channel_id=1, source_target_pairs={{0,64},{16,80},{32,96},{48,112},{64,0},{80,16},{96,32},{112,48},{1... | collective-permute-start | bytes 786440 | tf_op jit(solution)/shard_map/ppermute | solution.py:24
  38.7 30.2 %collective-permute-start.17 = (bf16[2,128,1024]{2,1,0:T(8,128)(2,1)S(1)}, bf16[2,128,1024]{2,1,0:T(8,128)(2,1)S(1)}, u32[]{:S(2)}, u32[]{:S(2)}) collective-permute-start(bf16[2,128,1024]{2,1,0:T(8,128)(2,1)S(1)} %get-tuple-element.54), channel_id=1, source_target_pairs={{0,64},{16,80},{32,96},{48,112},{64,0},{80,16},{96,32},{112,48},{1... | collective-permute-start | bytes 1572872 | tf_op jit(solution)/shard_map/ppermute | solution.py:24
  43.9 26.5 %collective-permute-start.19 = (bf16[2,128,1024]{2,1,0:T(8,128)(2,1)S(1)}, bf16[2,128,1024]{2,1,0:T(8,128)(2,1)S(1)}, u32[]{:S(2)}, u32[]{:S(2)}) collective-permute-start(bf16[2,128,1024]{2,1,0:T(8,128)(2,1)S(1)} %get-tuple-element.56), channel_id=1, source_target_pairs={{0,64},{16,80},{32,96},{48,112},{64,0},{80,16},{96,32},{112,48},{1... | collective-permute-start | bytes 1572872 | tf_op jit(solution)/shard_map/ppermute | solution.py:24
  53.3 28.3 %collective-permute-start.21 = (bf16[2,128,1024]{2,1,0:T(8,128)(2,1)S(1)}, bf16[2,128,1024]{2,1,0:T(8,128)(2,1)S(1)}, u32[]{:S(2)}, u32[]{:S(2)}) collective-permute-start(bf16[2,128,1024]{2,1,0:T(8,128)(2,1)S(1)} %get-tuple-element.58), channel_id=1, source_target_pairs={{0,64},{16,80},{32,96},{48,112},{64,0},{80,16},{96,32},{112,48},{1... | collective-permute-start | bytes 1572872 | tf_op jit(solution)/shard_map/ppermute | solution.py:24
  58.3 25.1 %collective-permute-start.6 = (bf16[2,2,128,768]{3,2,1,0:T(8,128)(2,1)S(1)}, bf16[2,2,128,768]{3,2,1,0:T(8,128)(2,1)S(1)}, u32[]{:S(2)}, u32[]{:S(2)}) collective-permute-start(bf16[2,2,128,768]{3,2,1,0:T(8,128)(2,1)S(1)} %gate_up.9), channel_id=1, source_target_pairs={{0,16},{16,32},{32,48},{48,0},{64,80},{80,96},{96,112},{112,64},{1... | collective-permute-start | bytes 2359304 | tf_op jit(solution)/shard_map/ppermute | solution.py:24
  63.4 23.2 %collective-permute-start.9 = (bf16[2,2,128,768]{3,2,1,0:T(8,128)(2,1)S(1)}, bf16[2,2,128,768]{3,2,1,0:T(8,128)(2,1)S(1)}, u32[]{:S(2)}, u32[]{:S(2)}) collective-permute-start(bf16[2,2,128,768]{3,2,1,0:T(8,128)(2,1)S(1)} %gate_up.10), channel_id=1, source_target_pairs={{0,48},{16,0},{32,16},{48,32},{64,112},{80,64},{96,80},{112,96},{1... | collective-permute-start | bytes 2359304 | tf_op jit(solution)/shard_map/ppermute | solution.py:24
  68.9 24.9 %collective-permute-start.12 = (bf16[2,2,128,768]{3,2,1,0:T(8,128)(2,1)S(1)}, bf16[2,2,128,768]{3,2,1,0:T(8,128)(2,1)S(1)}, u32[]{:S(2)}, u32[]{:S(2)}) collective-permute-start(bf16[2,2,128,768]{3,2,1,0:T(8,128)(2,1)S(1)} %gate_up.11), channel_id=1, source_target_pairs={{0,32},{16,48},{32,0},{48,16},{64,96},{80,112},{96,64},{112,80},{1... | collective-permute-start | bytes 2359304 | tf_op jit(solution)/shard_map/ppermute | solution.py:24
  69.4 24.4 %copy-start.2 = (bf16[1792,512]{1,0:T(8,128)(2,1)S(1)}, bf16[1792,512]{1,0:T(8,128)(2,1)}, u32[]{:S(2)}) copy-start(bf16[1792,512]{1,0:T(8,128)(2,1)} %rest_3_.5) | copy-start | bytes 5505028
  70.4 34.5 %collective-permute-start.16 = (bf16[2,128,1024]{2,1,0:T(8,128)(2,1)S(1)}, bf16[2,128,1024]{2,1,0:T(8,128)(2,1)S(1)}, u32[]{:S(2)}, u32[]{:S(2)}) collective-permute-start(bf16[2,128,1024]{2,1,0:T(8,128)(2,1)S(1)} %get-tuple-element.52), channel_id=1, source_target_pairs={{0,64},{16,80},{32,96},{48,112},{64,0},{80,16},{96,32},{112,48},{1... | collective-permute-start | bytes 1572872 | tf_op jit(solution)/shard_map/ppermute | solution.py:24
  81.6 25.4 %collective-permute-start.18 = (bf16[2,128,1024]{2,1,0:T(8,128)(2,1)S(1)}, bf16[2,128,1024]{2,1,0:T(8,128)(2,1)S(1)}, u32[]{:S(2)}, u32[]{:S(2)}) collective-permute-start(bf16[2,128,1024]{2,1,0:T(8,128)(2,1)S(1)} %add_convert_fusion.2), channel_id=1, source_target_pairs={{0,16},{16,32},{32,48},{48,0},{64,80},{80,96},{96,112},{112,64},{1... | collective-permute-start | bytes 1572872 | tf_op jit(solution)/shard_map/ppermute | solution.py:24
  83.4 27.6 %collective-permute-start.20 = (bf16[2,128,1024]{2,1,0:T(8,128)(2,1)S(1)}, bf16[2,128,1024]{2,1,0:T(8,128)(2,1)S(1)}, u32[]{:S(2)}, u32[]{:S(2)}) collective-permute-start(bf16[2,128,1024]{2,1,0:T(8,128)(2,1)S(1)} %add_convert_fusion.1), channel_id=1, source_target_pairs={{0,48},{16,0},{32,16},{48,32},{64,112},{80,64},{96,80},{112,96},{1... | collective-permute-start | bytes 1572872 | tf_op jit(solution)/shard_map/ppermute | solution.py:24
  86.6 29.7 %collective-permute-start.22 = (bf16[2,128,1024]{2,1,0:T(8,128)(2,1)S(1)}, bf16[2,128,1024]{2,1,0:T(8,128)(2,1)S(1)}, u32[]{:S(2)}, u32[]{:S(2)}) collective-permute-start(bf16[2,128,1024]{2,1,0:T(8,128)(2,1)S(1)} %add_convert_fusion), channel_id=1, source_target_pairs={{0,32},{16,48},{32,0},{48,16},{64,96},{80,112},{96,64},{112,80},{1... | collective-permute-start | bytes 1572872 | tf_op jit(solution)/shard_map/ppermute | solution.py:24
  93.8 39.5 %collective-permute-start.25 = (bf16[1792,512]{1,0:T(8,128)(2,1)S(1)}, bf16[1792,512]{1,0:T(8,128)(2,1)S(1)}, u32[]{:S(2)}, u32[]{:S(2)}) collective-permute-start(bf16[1792,512]{1,0:T(8,128)(2,1)S(1)} %copy-done.2), channel_id=1, source_target_pairs={{0,8},{8,0},{1,9},{9,1},{2,10},{10,2},{3,11},{11,3},{4,12},{12,4},... | collective-permute-start | bytes 5505032 | tf_op jit(solution)/shard_map/ppermute | solution.py:264
  104.9 19.5 %collective-permute-start.13 = (bf16[2,128,768]{2,1,0:T(8,128)(2,1)S(1)}, bf16[2,128,768]{2,1,0:T(8,128)(2,1)S(1)}, u32[]{:S(2)}, u32[]{:S(2)}) collective-permute-start(bf16[2,128,768]{2,1,0:T(8,128)(2,1)S(1)} %fusion.2), channel_id=1, source_target_pairs={{0,64},{16,80},{32,96},{48,112},{64,0},{80,16},{96,32},{112,48},{1... | collective-permute-start | bytes 1179656 | tf_op jit(solution)/shard_map/ppermute | solution.py:24
  117.0 21.1 %collective-permute-start.32 = (bf16[128,1024]{1,0:T(8,128)(2,1)S(1)}, bf16[128,1024]{1,0:T(8,128)(2,1)S(1)}, u32[]{:S(2)}, u32[]{:S(2)}) collective-permute-start(bf16[128,1024]{1,0:T(8,128)(2,1)S(1)} %fusion.1.rest_2_), channel_id=1, source_target_pairs={{0,64},{16,80},{32,96},{48,112},{64,0},{80,16},{96,32},{112,48},{1... | collective-permute-start | bytes 786440 | tf_op jit(solution)/shard_map/ppermute | solution.py:24
  117.2 20.9 %collective-permute-start.30 = (bf16[128,1024]{1,0:T(8,128)(2,1)S(1)}, bf16[128,1024]{1,0:T(8,128)(2,1)S(1)}, u32[]{:S(2)}, u32[]{:S(2)}) collective-permute-start(bf16[128,1024]{1,0:T(8,128)(2,1)S(1)} %fusion.1.rest_2_), channel_id=1, source_target_pairs={{0,48},{16,0},{32,16},{48,32},{64,112},{80,64},{96,80},{112,96},{1... | collective-permute-start | bytes 786440 | tf_op jit(solution)/shard_map/ppermute | solution.py:24
  124.4 13.9 %collective-permute-start.27 = (bf16[128,1024]{1,0:T(8,128)(2,1)S(1)}, bf16[128,1024]{1,0:T(8,128)(2,1)S(1)}, u32[]{:S(2)}, u32[]{:S(2)}) collective-permute-start(bf16[128,1024]{1,0:T(8,128)(2,1)S(1)} %fusion.1.rest_2_), channel_id=1, source_target_pairs={{0,16},{16,32},{32,48},{48,0},{64,80},{80,96},{96,112},{112,64},{1... | collective-permute-start | bytes 786440 | tf_op jit(solution)/shard_map/ppermute | solution.py:24
  124.7 8.5 %collective-permute-start.14 = (bf16[128,768]{1,0:T(8,128)(2,1)S(1)}, bf16[128,768]{1,0:T(8,128)(2,1)S(1)}, u32[]{:S(2)}, u32[]{:S(2)}) collective-permute-start(bf16[128,768]{1,0:T(8,128)(2,1)S(1)} %fusion.3.rest_0_), channel_id=1, source_target_pairs={{0,64},{16,80},{32,96},{48,112},{64,0},{80,16},{96,32},{112,48},{1... | collective-permute-start | bytes 589832 | tf_op jit(solution)/shard_map/ppermute | solution.py:24
  133.2 6.8 %collective-permute-start.23 = (bf16[128,1024]{1,0:T(8,128)(2,1)S(1)}, bf16[128,1024]{1,0:T(8,128)(2,1)S(1)}, u32[]{:S(2)}, u32[]{:S(2)}) collective-permute-start(bf16[128,1024]{1,0:T(8,128)(2,1)S(1)} %fusion.1.rest_2_), channel_id=1, source_target_pairs={{0,32},{16,48},{32,0},{48,16},{64,96},{80,112},{96,64},{112,80},{1... | collective-permute-start | bytes 786440 | tf_op jit(solution)/shard_map/ppermute | solution.py:24
  133.3 17.0 %collective-permute-start.29 = (bf16[2,128,768]{2,1,0:T(8,128)(2,1)S(1)}, bf16[2,128,768]{2,1,0:T(8,128)(2,1)S(1)}, u32[]{:S(2)}, u32[]{:S(2)}) collective-permute-start(bf16[2,128,768]{2,1,0:T(8,128)(2,1)S(1)} %pad_maximum_fusion), channel_id=1, source_target_pairs={{0,48},{16,0},{32,16},{48,32},{64,112},{80,64},{96,80},{112,96},{1... | collective-permute-start | bytes 1179656 | tf_op jit(solution)/shard_map/ppermute | solution.py:24
  138.1 7.0 %collective-permute-start.31 = (bf16[128,1024]{1,0:T(8,128)(2,1)S(1)}, bf16[128,1024]{1,0:T(8,128)(2,1)S(1)}, u32[]{:S(2)}, u32[]{:S(2)}) collective-permute-start(bf16[128,1024]{1,0:T(8,128)(2,1)S(1)} %collective-permute-done.30.rest_1_), channel_id=1, source_target_pairs={{0,64},{16,80},{32,96},{48,112},{64,0},{80,16},{96,32},{112,48},{1... | collective-permute-start | bytes 786440 | tf_op jit(solution)/shard_map/ppermute | solution.py:24
  138.1 14.2 %collective-permute-start.26 = (bf16[2,128,768]{2,1,0:T(8,128)(2,1)S(1)}, bf16[2,128,768]{2,1,0:T(8,128)(2,1)S(1)}, u32[]{:S(2)}, u32[]{:S(2)}) collective-permute-start(bf16[2,128,768]{2,1,0:T(8,128)(2,1)S(1)} %pad_maximum_fusion), channel_id=1, source_target_pairs={{0,16},{16,32},{32,48},{48,0},{64,80},{80,96},{96,112},{112,64},{1... | collective-permute-start | bytes 1179656 | tf_op jit(solution)/shard_map/ppermute | solution.py:24
  138.3 19.5 %collective-permute-start.15 = (bf16[2,128,768]{2,1,0:T(8,128)(2,1)S(1)}, bf16[2,128,768]{2,1,0:T(8,128)(2,1)S(1)}, u32[]{:S(2)}, u32[]{:S(2)}) collective-permute-start(bf16[2,128,768]{2,1,0:T(8,128)(2,1)S(1)} %pad_maximum_fusion), channel_id=1, source_target_pairs={{0,32},{16,48},{32,0},{48,16},{64,96},{80,112},{96,64},{112,80},{1... | collective-permute-start | bytes 1179656 | tf_op jit(solution)/shard_map/ppermute | solution.py:24
  140.0 12.2 %collective-permute-start.28 = (bf16[128,1024]{1,0:T(8,128)(2,1)S(1)}, bf16[128,1024]{1,0:T(8,128)(2,1)S(1)}, u32[]{:S(2)}, u32[]{:S(2)}) collective-permute-start(bf16[128,1024]{1,0:T(8,128)(2,1)S(1)} %collective-permute-done.27.rest_1_), channel_id=1, source_target_pairs={{0,64},{16,80},{32,96},{48,112},{64,0},{80,16},{96,32},{112,48},{1... | collective-permute-start | bytes 786440 | tf_op jit(solution)/shard_map/ppermute | solution.py:24
  145.1 10.5 %collective-permute-start.24 = (bf16[128,1024]{1,0:T(8,128)(2,1)S(1)}, bf16[128,1024]{1,0:T(8,128)(2,1)S(1)}, u32[]{:S(2)}, u32[]{:S(2)}) collective-permute-start(bf16[128,1024]{1,0:T(8,128)(2,1)S(1)} %collective-permute-done.23.rest_1_), channel_id=1, source_target_pairs={{0,64},{16,80},{32,96},{48,112},{64,0},{80,16},{96,32},{112,48},{1... | collective-permute-start | bytes 786440 | tf_op jit(solution)/shard_map/ppermute | solution.py:24
